TPU v7x, 32 devices: a whole 2x2x4 slice. The times are simulated.
32 devices in a mesh: batch: 8 (over z, y), mp: 4 (over x, core).
Axes of the slice: x: 2, y: 2, z: 4, core: 2. Of those that a mesh axis runs over, the one named last changes fastest.
Arguments:
- lookup_ids: int32 [64, 16384], P('batch'), may hold values from 0 to 8191
- table_feature: int32 [64], replicated, may hold values from 0 to 63, each once
- tables: bfloat16 [64, 8192, 128], P('batch'), may hold values from -6 to 6
- cross_down: bfloat16 [2, 8192, 512], P(None, 'mp'), may hold values from -0.0625 to 0.0625
- cross_up: bfloat16 [2, 512, 8192], P(None, None, 'mp'), may hold values from -0.25 to 0.25
- cross_bias: float32 [2, 8192], P(None, 'mp'), may hold values from -3 to 3
Outputs:
- crossed: bfloat16 [16384, 8192], P('batch', 'mp')
Inputs may be any that keep to these rules, and one draw needn't show every extreme that they name: `table_feature`: each number appears once.
All inputs are finite; a program needn't handle non-finite values.
Results may differ from a plain program's by a relative error of at most 0.015.
Values may be sent and summed in bfloat16 or wider, within the bound.
No kernel may reach another device: no remote copies, remote signals or barrier semaphores. Data moves between devices by JAX's collectives and lax.ppermute only.
A program may use at most 128 MiB of HBM per device.

v0:
```python
import functools

import jax
import jax.numpy as jnp
from jax import lax
from jax.experimental import pallas as pl
from jax.experimental.pallas import tpu as pltpu
from jax.sharding import PartitionSpec as P


PLAN = ((3, True), (3, False), (2, False))
UNROLL = 32
WIDEN = 1024
MIX = 32
MIB = 2**20


def gather_kernel(by_owner, place_ref, idx_ref, table_ref, *refs):
    outs, (wide, stage) = refs[:-2], refs[-2:]
    slots, count, emb = stage.shape
    turn = pl.program_id(0)
    rows = wide.shape[0]
    lanes = emb // slots
    halves = outs[0].shape[-1] // emb
    parts = slots // halves

    def widen(i, carry):
        at = pl.multiple_of(i * WIDEN, WIDEN)
        wide[pl.ds(at, WIDEN), :] = table_ref[0, pl.ds(at, WIDEN), :].astype(jnp.float32)
        return carry

    lax.fori_loop(0, rows // WIDEN, widen, 0)

    def fetch(i, carry):
        at = pl.multiple_of(i * UNROLL, UNROLL)
        for u in range(UNROLL):
            row = idx_ref[0, 0, at + u]
            stage[turn, pl.ds(at + u, 1), :] = wide[pl.ds(row, 1), :]
        return carry

    lax.fori_loop(0, count // UNROLL, fetch, 0)

    @pl.when(turn == slots - 1)
    def _():
        group = lax.broadcasted_iota(jnp.int32, (MIX, emb), 1) // lanes
        masks = [
            group == lax.rem(place_ref[0] * halves + u, slots) for u in range(slots)
        ]

        def mixed(at):
            turned = [stage[0, pl.ds(at, MIX), :]]
            for t in range(1, slots):
                turned.append(pltpu.roll(stage[t, pl.ds(at, MIX), :], t * lanes, 1))
            for j in range(parts):
                for h in range(halves):
                    value = turned[-1]
                    for t in range(slots - 1):
                        value = jnp.where(
                            masks[(j * halves + h + t) % slots], turned[t], value
                        )
                    yield j, slice(h * emb, (h + 1) * emb), value.astype(outs[0].dtype)

        if by_owner:
            share = count // len(outs)
            for k, out in enumerate(outs):

                def mix(i, carry):
                    at = pl.multiple_of(i * MIX, MIX)
                    for j, columns, value in mixed(k * share + at):
                        out[j, pl.ds(at, MIX), columns] = value
                    return carry

                lax.fori_loop(0, share // MIX, mix, 0)
        else:

            def mix(i, carry):
                at = pl.multiple_of(i * MIX, MIX)
                for j, columns, value in mixed(at):
                    outs[j][pl.ds(at, MIX), columns] = value
                return carry

            lax.fori_loop(0, count // MIX, mix, 0)


def halves_of(slots, parts, emb):
    if slots % parts or emb % 128 or emb % slots:
        return 0
    return slots // parts


def gather(place, ids, tables, parts, by_owner):
    slots, rows, emb = tables.shape
    owners, part_rows = ids.shape[1:]
    count = owners * part_rows
    lanes = emb // parts
    width = slots * lanes
    if not halves_of(slots, parts, emb):
        looked = jnp.stack(
            [jnp.take(tables[s], ids[s].reshape(-1), axis=0) for s in range(slots)], axis=1
        ).reshape(count, slots, parts, lanes)
        looked = jnp.transpose(looked, (2, 0, 1, 3)).reshape(parts, count, width)
        looked = jnp.concatenate([looked, looked], axis=0)
        looked = lax.dynamic_slice_in_dim(looked, place[0], parts, 0)
        looked = looked.reshape(parts, owners, part_rows, width)
        if by_owner:
            return [looked[:, k] for k in range(owners)]
        return [looked[j] for j in range(parts)]
    if by_owner:
        shapes = [(parts, part_rows, width)] * owners
        out_specs = [pl.BlockSpec(shape, lambda s, p: (0, 0, 0)) for shape in shapes]
    else:
        shapes = [(count, width)] * parts
        out_specs = [pl.BlockSpec(shape, lambda s, p: (0, 0)) for shape in shapes]
    outs = pl.pallas_call(
        functools.partial(gather_kernel, by_owner),
        grid_spec=pltpu.PrefetchScalarGridSpec(
            num_scalar_prefetch=1,
            grid=(slots,),
            in_specs=[
                pl.BlockSpec((1, 1, count), lambda s, p: (s, 0, 0), memory_space=pltpu.SMEM),
                pl.BlockSpec((1, rows, emb), lambda s, p: (s, 0, 0)),
            ],
            out_specs=out_specs,
            scratch_shapes=[
                pltpu.VMEM((rows, emb), jnp.float32),
                pltpu.VMEM((slots, count, emb), jnp.float32),
            ],
        ),
        out_shape=[jax.ShapeDtypeStruct(shape, tables.dtype) for shape in shapes],
        compiler_params=pltpu.CompilerParams(vmem_limit_bytes=60 * MIB),
        cost_estimate=pl.CostEstimate(
            flops=1000, bytes_accessed=slots * rows * emb * 2, transcendentals=0
        ),
        name="gather",
    )(place, ids.reshape(slots, 1, count), tables)
    if by_owner:
        return outs
    return [out.reshape(owners, part_rows, width) for out in outs]


def swap_kernel(count, *refs):
    for a, source in enumerate(refs[:count]):
        for b, target in enumerate(refs[count:]):
            target[a] = source[b]


def swap(arrays):
    inner, part_rows, width = arrays[0].shape
    count = len(arrays)
    if width % 128:
        return [jnp.stack([array[b] for array in arrays]) for b in range(inner)]
    spec = pl.BlockSpec(memory_space=pltpu.VMEM)
    return pl.pallas_call(
        functools.partial(swap_kernel, count),
        in_specs=[spec] * count,
        out_specs=[spec] * inner,
        out_shape=[jax.ShapeDtypeStruct((count, part_rows, width), arrays[0].dtype)] * inner,
        compiler_params=pltpu.CompilerParams(vmem_limit_bytes=60 * MIB),
        cost_estimate=pl.CostEstimate(
            flops=1000, bytes_accessed=4 * inner * count * part_rows * width, transcendentals=0
        ),
        name="swap",
    )(*arrays)


def project_kernel(by_owner, tile, place_ref, weight_ref, *refs):
    pieces, (x_ref, term_ref) = refs[:-2], refs[-2:]
    if by_owner:
        groups, (owners, part_rows, width) = len(pieces), pieces[0].shape
    else:
        owners, (groups, part_rows, width) = len(pieces), pieces[0].shape
    halves = x_ref.shape[0]
    wide = width // halves
    for j in range(groups):
        source = lax.rem(place_ref[0] + groups - j, groups)
        at = pl.multiple_of(source * part_rows, part_rows)
        for k in range(owners):
            piece = pieces[j][k] if by_owner else pieces[k][j]
            for h in range(halves):
                x_ref[h, pl.ds(at, part_rows), k * wide : (k + 1) * wide] = piece[
                    :, h * wide : (h + 1) * wide
                ]

    def body(i, carry):
        at = pl.multiple_of(i * tile, tile)
        total = jnp.zeros((tile, weight_ref.shape[2]), jnp.float32)
        for h in range(halves):
            total = total + jnp.dot(
                x_ref[h, pl.ds(at, tile), :], weight_ref[h], preferred_element_type=jnp.float32
            )
        term_ref[pl.ds(at, tile), :] = total.astype(term_ref.dtype)
        return carry

    lax.fori_loop(0, x_ref.shape[1] // tile, body, 0)


def project(place, pieces, weight, by_owner):
    if by_owner:
        groups, (owners, part_rows, width) = len(pieces), pieces[0].shape
    else:
        owners, (groups, part_rows, width) = len(pieces), pieces[0].shape
    halves, half_width, rank = weight.shape
    rows = groups * part_rows
    if width % 128:
        parts = [
            jnp.concatenate(
                [pieces[j][k] if by_owner else pieces[k][j] for k in range(owners)], axis=1
            )
            for j in range(groups)
        ]
        parts = parts[:1] + parts[:0:-1]
        x = jnp.stack(parts + parts)
        start = (groups - place[0]) % groups
        x = lax.dynamic_slice_in_dim(x, start, groups, 0).reshape(1, rows, half_width)
        term = jnp.dot(x[0], weight[0], preferred_element_type=jnp.float32)
        return x, term.astype(jnp.bfloat16)
    spec = pl.BlockSpec(memory_space=pltpu.VMEM)
    return pl.pallas_call(
        functools.partial(project_kernel, by_owner, min(256, rows)),
        in_specs=[pl.BlockSpec(memory_space=pltpu.SMEM)] + [spec] * (len(pieces) + 1),
        out_specs=[spec] * 2,
        out_shape=[
            jax.ShapeDtypeStruct((halves, rows, half_width), weight.dtype),
            jax.ShapeDtypeStruct((rows, rank), weight.dtype),
        ],
        compiler_params=pltpu.CompilerParams(vmem_limit_bytes=60 * MIB),
        cost_estimate=pl.CostEstimate(
            flops=1000,
            bytes_accessed=4 * rows * halves * half_width,
            transcendentals=0,
        ),
        name="project",
    )(place, weight, *pieces)


def arrange_kernel(x_ref, placing_ref, out_ref):
    out_ref[...] = jnp.dot(
        x_ref[0], placing_ref[0], preferred_element_type=jnp.float32
    ).astype(out_ref.dtype)


def arrange(x, placing):
    halves, rows, half_width = x.shape
    tile = 256
    if half_width % 128 or rows % tile:
        parts = [
            jnp.dot(x[h], placing[h], preferred_element_type=jnp.float32).astype(x.dtype)
            for h in range(halves)
        ]
        return jnp.concatenate(parts, axis=1)
    return pl.pallas_call(
        arrange_kernel,
        grid=(halves, rows // tile),
        in_specs=[
            pl.BlockSpec((1, tile, half_width), lambda h, i: (h, i, 0)),
            pl.BlockSpec((1, half_width, half_width), lambda h, i: (h, 0, 0)),
        ],
        out_specs=pl.BlockSpec((tile, half_width), lambda h, i: (i, h)),
        out_shape=jax.ShapeDtypeStruct((rows, halves * half_width), x.dtype),
        compiler_params=pltpu.CompilerParams(vmem_limit_bytes=60 * MIB),
        cost_estimate=pl.CostEstimate(
            flops=1000,
            bytes_accessed=4 * rows * halves * half_width,
            transcendentals=0,
        ),
        name="arrange",
    )(x, placing)


def last_kernel(low_ref, up_ref, bias_ref, embedded_ref, state_ref, *refs):
    out_ref = refs[-1]
    high = jnp.dot(low_ref[0], up_ref[...], preferred_element_type=jnp.float32) + bias_ref[...]
    value = embedded_ref[0].astype(jnp.float32) * high + state_ref[0].astype(jnp.float32)
    out_ref[0] = value.astype(out_ref.dtype)


def last(low, up, bias, embedded, state, start, shape, out):
    groups, _, width = shape
    part_rows = low.shape[0] // groups
    rank = low.shape[1]
    tile = part_rows
    while start % tile or tile > 256:
        tile //= 2
    row_spec = lambda size: pl.BlockSpec((1, tile, size), lambda j, i: (j, i, 0))
    operands = [
        low.reshape(groups, part_rows, rank),
        up,
        bias[None, :],
        embedded.reshape(groups, part_rows, width),
        state.reshape(groups, part_rows, width),
    ]
    in_specs = [
        row_spec(rank),
        pl.BlockSpec((rank, width), lambda j, i: (0, 0)),
        pl.BlockSpec((1, width), lambda j, i: (0, 0)),
        row_spec(width),
        row_spec(width),
    ]
    aliases = {}
    if out is not None:
        aliases = {len(operands): 0}
        operands.append(out)
        in_specs.append(pl.BlockSpec(memory_space=pl.ANY))
    rows = groups * part_rows
    return pl.pallas_call(
        last_kernel,
        grid=(groups, part_rows // tile),
        in_specs=in_specs,
        out_specs=pl.BlockSpec((1, tile, width), lambda j, i: (j, start // tile + i, 0)),
        out_shape=jax.ShapeDtypeStruct(shape, jnp.bfloat16),
        input_output_aliases=aliases,
        compiler_params=pltpu.CompilerParams(vmem_limit_bytes=60 * MIB),
        cost_estimate=pl.CostEstimate(
            flops=1000, bytes_accessed=6 * rows * width, transcendentals=0
        ),
        name="last",
    )(*operands)


def spread(arrays, axis):
    size = len(arrays)
    moved = [arrays[0]]
    for step in range(1, size):
        pairs = [(i, (i + step) % size) for i in range(size)]
        moved.append(lax.ppermute(arrays[step], axis, pairs))
    return moved


def trade(value, axis, step):
    size = lax.axis_size(axis)
    return lax.ppermute(value, axis, [(i, i ^ step) for i in range(size)])


def add(one, other):
    return (one.astype(jnp.float32) + other.astype(jnp.float32)).astype(one.dtype)


def sum_over(term, axis):
    size = lax.axis_size(axis)
    rows = term.shape[0]
    if size & (size - 1) or size < 2 or rows % 32:
        return lax.psum(term, axis)
    half = rows // 2
    odd = lax.axis_index(axis) % 2
    kept = lax.dynamic_slice_in_dim(term, odd * half, half)
    given = lax.dynamic_slice_in_dim(term, (1 - odd) * half, half)
    kept = add(kept, trade(given, axis, 1))
    step = 2
    while step < size:
        kept = add(kept, trade(kept, axis, step))
        step *= 2
    other = trade(kept, axis, 1)
    return jnp.where(
        odd == 0,
        jnp.concatenate([kept, other], axis=0),
        jnp.concatenate([other, kept], axis=0),
    )


def tie(value, others):
    return lax.optimization_barrier((value, others))


def stages(lookup_ids, table_feature, tables, cross_down, cross_up, cross_bias):
    slots, _, emb = tables.shape
    feats = table_feature.shape[0]
    owners, groups = lax.axis_size("batch"), lax.axis_size("mp")
    owner, member = lax.axis_index("batch"), lax.axis_index("mp")
    examples = lookup_ids.shape[1] // owners
    share = examples // groups
    lanes = emb // groups
    width = feats * lanes
    place = member.astype(jnp.int32)[None]
    wanted = lookup_ids.reshape(slots, owners, groups, share)
    wanted = lax.dynamic_index_in_dim(wanted, member, 2, keepdims=False)
    wanted = lax.dynamic_slice_in_dim(
        jnp.concatenate([wanted, wanted], axis=1), owner, owners, 1
    )

    unit = share // sum(size for size, _ in PLAN)
    starts, sizes, at = [], [], 0
    for size, _ in PLAN:
        starts.append(at)
        sizes.append(size * unit)
        at += size * unit

    held = []
    for (size, owner_first), begin, rows in zip(PLAN, starts, sizes):
        part = wanted[:, :, begin : begin + rows]
        if held:
            part, _ = tie(part, held[-1][0])
        found = gather(place, part, tables, groups, owner_first)
        if owner_first:
            moved = spread(found, "batch")
        else:
            moved = spread(found, "mp")
        held.append((found, moved))

    table_feature, _ = tie(table_feature, held[-1][0])
    halves = halves_of(slots, groups, emb) or 1
    step = lanes // halves
    source = (owner + owners - jnp.arange(owners)) % owners
    spot = jnp.arange(slots)[None, :]
    if halves_of(slots, groups, emb):
        spot = (spot + slots - member * halves - jnp.arange(halves)[:, None]) % slots
    feature = table_feature[source[None, :, None] * slots + spot[:, None, :]]
    column = feature[:, :, :, None] + jnp.arange(step) * feats
    column = column.reshape(halves, width // halves)
    placing = (column[:, :, None] == jnp.arange(width // halves)).astype(jnp.bfloat16)
    placing = lax.optimization_barrier(placing)
    down_first = jnp.einsum(
        "hcd,hdr->hcr",
        placing,
        cross_down[0].reshape(halves, width // halves, -1),
        preferred_element_type=jnp.float32,
    )
    down_first = lax.optimization_barrier(down_first.astype(jnp.bfloat16))

    pieces_of = {}
    previous = down_first
    for c in sorted(range(len(PLAN)), key=lambda c: (c != 1, c)):
        owner_first, moved = PLAN[c][1], held[c][1]
        moved, _ = tie(moved, previous)
        sent = swap(moved)
        previous = sent
        if owner_first:
            pieces_of[c] = spread(sent, "mp")
        else:
            pieces_of[c] = spread(sent, "batch")

    out = finish = None
    for c, ((size, owner_first), begin, rows) in enumerate(zip(PLAN, starts, sizes)):
        final = c == len(PLAN) - 1
        pieces, _ = tie(pieces_of[c], previous)
        x, term = project(place, pieces, down_first, owner_first)
        if final and finish is not None:
            out = finish(out)
            x, out = tie(x, out)
        embedded = arrange(x, placing)
        previous = embedded
        state = embedded
        layers = cross_down.shape[0]
        for layer in range(layers):
            if layer:
                term = jnp.dot(state, cross_down[layer], preferred_element_type=jnp.float32)
                term = term.astype(jnp.bfloat16)
                if c == len(PLAN) - 2:
                    previous = term
            low = sum_over(term, "mp")
            if layer < layers - 1:
                high = (
                    jnp.dot(low, cross_up[layer], preferred_element_type=jnp.float32)
                    + cross_bias[layer][None, :]
                )
                state = (
                    embedded.astype(jnp.float32) * high + state.astype(jnp.float32)
                ).astype(jnp.bfloat16)
            else:
                if finish is not None and not final:
                    out = finish(out)
                finish = functools.partial(
                    last,
                    low,
                    cross_up[layer],
                    cross_bias[layer],
                    embedded,
                    state,
                    begin,
                    (groups, share, width),
                )
    out = finish(out)
    return out.reshape(examples, width)


def solution(mesh):
    return jax.shard_map(
        stages,
        mesh=mesh,
        in_specs=(
            P("batch", None),
            P(),
            P("batch", None, None),
            P(None, "mp", None),
            P(None, None, "mp"),
            P(None, "mp"),
        ),
        out_specs=P("batch", "mp"),
        check_vma=False,
    )
```

profile of v0, /device:TPU:0, one launch (start us, length us, event | category | flops | bytes accessed | tf_op | source)
XLA Modules:
  0.0 368.4 jit_solution(12625869840894716498)
XLA Ops:
  2.0 23.0 %gather.9 = (bf16[4,192,256]{2,1,0:T(8,128)(2,1)}, bf16[4,192,256]{2,1,0:T(8,128)(2,1)}, bf16[4,192,256]{2,1,0:T(8,128)(2,1)}, bf16[4,192,256]{2,1,0:T(8,128)(2,...) custom-call(s32[1]{0:T(128)} %bitcast.place_ref, ...), custom_call_target="tpu_custom_call" | custom-call | flops 1000 | bytes 16777216 | tf_op jit(solution)/shard_map/gather/pallas_call | solution.py:114
  32.9 23.0 %gather.10 = (bf16[1536,256]{1,0:T(8,128)(2,1)}, bf16[1536,256]{1,0:T(8,128)(2,1)}, bf16[1536,256]{1,0:T(8,128)(2,1)}, bf16[1536,256]{1,0:T(8,128)(2,1)}) custom-call(s32[1]{0:T(128)} %bitcast.place_ref, s32[8,1,1536]{2,1,0:T(1,128)} %reshape.157.idx_ref, bf16[8,8192,128]{2,1,0:T(8,128)(2,1)} %table_ref.5), custom_call_target="tpu_custom_call" | custom-call | flops 1000 | bytes 16777216 | tf_op jit(solution)/shard_map/gather/pallas_call | solution.py:114
  59.6 18.0 %gather.11 = (bf16[1024,256]{1,0:T(8,128)(2,1)}, bf16[1024,256]{1,0:T(8,128)(2,1)}, bf16[1024,256]{1,0:T(8,128)(2,1)}, bf16[1024,256]{1,0:T(8,128)(2,1)}) custom-call(s32[1]{0:T(128)} %bitcast.place_ref, s32[8,1,1024]{2,1,0:T(1,128)} %bitcast.73, bf16[8,8192,128]{2,1,0:T(8,128)(2,1)} %table_ref.5), custom_call_target="tpu_custom_call" | custom-call | flops 1000 | bytes 16777216 | tf_op jit(solution)/shard_map/gather/pallas_call | solution.py:114
  84.6 23.0 %collective-permute-done.6.refs_4_ = bf16[4,192,256]{2,1,0:T(8,128)(2,1)S(1)} collective-permute-done((bf16[4,192,256]{2,1,0:T(8,128)(2,1)}, bf16[4,192,256]{2,1,0:T(8,128)(2,1)S(1)}, u32[]{:S(2)}, u32[]{:S(2)}) %collective-permute-start.6) | collective-permute-done | bytes 393248 | tf_op jit(solution)/shard_map/ppermute | solution.py:325
  110.1 17.7 %collective-permute-start.9 = (bf16[4,192,256]{2,1,0:T(8,128)(2,1)}, bf16[4,192,256]{2,1,0:T(8,128)(2,1)}, u32[]{:S(2)}, u32[]{:S(2)}) collective-permute-start(bf16[4,192,256]{2,1,0:T(8,128)(2,1)} %get-tuple-element.95), channel_id=1, source_target_pairs={{0,28},{4,0},{8,4},{12,8},{16,12},{20,16},{24,20},{28,24},{1,29},{... | collective-permute-start | bytes 1179656 | tf_op jit(solution)/shard_map/ppermute | solution.py:325
  143.8 9.4 %collective-permute-done.2.refs_3_ = bf16[8,128,256]{2,1,0:T(8,128)(2,1)} collective-permute-done((bf16[8,128,256]{2,1,0:T(8,128)(2,1)}, bf16[8,128,256]{2,1,0:T(8,128)(2,1)}, u32[]{:S(2)}, u32[]{:S(2)}) %collective-permute-start.2) | collective-permute-done | bytes 524320 | tf_op jit(solution)/shard_map/ppermute | solution.py:325
  157.2 9.8 %collective-permute-done.21.refs_2_ = bf16[4,192,256]{2,1,0:T(8,128)(2,1)} collective-permute-done((bf16[4,192,256]{2,1,0:T(8,128)(2,1)}, bf16[4,192,256]{2,1,0:T(8,128)(2,1)}, u32[]{:S(2)}, u32[]{:S(2)}) %collective-permute-start.21) | collective-permute-done | bytes 393248 | tf_op jit(solution)/shard_map/ppermute | solution.py:325
  171.0 15.2 %collective-permute-done.29.refs_3_ = bf16[8,192,256]{2,1,0:T(8,128)(2,1)S(1)} collective-permute-done((bf16[8,192,256]{2,1,0:T(8,128)(2,1)}, bf16[8,192,256]{2,1,0:T(8,128)(2,1)S(1)}, u32[]{:S(2)}, u32[]{:S(2)}) %collective-permute-start.29) | collective-permute-done | bytes 786464 | tf_op jit(solution)/shard_map/ppermute | solution.py:325
  187.1 6.7 %project.3 = (bf16[2,768,1024]{2,1,0:T(8,128)(2,1)}, bf16[768,512]{1,0:T(8,128)(2,1)}) custom-call(s32[1]{0:T(128)} %bitcast.place_ref, bf16[2,1024,512]{2,1,0:T(8,128)(2,1)} %convolution_convert_fusion.weight_ref, bf16[8,192,256]{2,1,0:T(8,128)(2,1)} %get-tuple-element.143.refs_0_, bf16[8,192,256]{2,1,0:T(8,128)(2,1)} %copy-done.17, ...), custom_call_target="tpu_custom_call" | custom-call | flops 1000 | bytes 6291456 | tf_op jit(solution)/shard_map/project/pallas_call | solution.py:218
  198.4 8.8 %arrange.3 = bf16[768,2048]{1,0:T(8,128)(2,1)} custom-call(bf16[2,768,1024]{2,1,0:T(8,128)(2,1)} %get-tuple-element.147.x_ref, bf16[2,1024,1024]{2,1,0:T(8,128)(2,1)} %copy-done.3), custom_call_target="tpu_custom_call" | custom-call | flops 1000 | bytes 6291456 | tf_op jit(solution)/shard_map/arrange/pallas_call | solution.py:251
  207.9 6.6 %project.4 = (bf16[2,768,1024]{2,1,0:T(8,128)(2,1)}, bf16[768,512]{1,0:T(8,128)(2,1)}) custom-call(s32[1]{0:T(128)} %bitcast.place_ref, bf16[2,1024,512]{2,1,0:T(8,128)(2,1)} %convolution_convert_fusion.weight_ref, bf16[4,192,256]{2,1,0:T(8,128)(2,1)} %get-tuple-element.148.refs_0_, bf16[4,192,256]{2,1,0:T(8,128)(2,1)} %collective-permute-done.20.refs_1_, ...), custom_call_target="tpu_custom_call" | custom-call | flops 1000 | bytes 6291456 | tf_op jit(solution)/shard_map/project/pallas_call | solution.py:218
  221.2 8.8 %collective-permute-done.37 = bf16[384,512]{1,0:T(8,128)(2,1)S(1)} collective-permute-done((bf16[384,512]{1,0:T(8,128)(2,1)S(1)}, bf16[384,512]{1,0:T(8,128)(2,1)S(1)}, u32[]{:S(2)}, u32[]{:S(2)}) %collective-permute-start.37) | collective-permute-done | bytes 393248 | tf_op jit(solution)/shard_map/ppermute | solution.py:331
  230.8 5.7 %collective-permute-start.13 = (bf16[4,128,256]{2,1,0:T(8,128)(2,1)}, bf16[4,128,256]{2,1,0:T(8,128)(2,1)}, u32[]{:S(2)}, u32[]{:S(2)}) collective-permute-start(bf16[4,128,256]{2,1,0:T(8,128)(2,1)} %get-tuple-element.136), channel_id=1, source_target_pairs={{0,4},{4,8},{8,12},{12,16},{16,20},{20,24},{24,28},{28,0},{1,5},{5... | collective-permute-start | bytes 786440 | tf_op jit(solution)/shard_map/ppermute | solution.py:325
  236.5 12.5 %collective-permute-start.14 = (bf16[4,128,256]{2,1,0:T(8,128)(2,1)}, bf16[4,128,256]{2,1,0:T(8,128)(2,1)}, u32[]{:S(2)}, u32[]{:S(2)}) collective-permute-start(bf16[4,128,256]{2,1,0:T(8,128)(2,1)} %get-tuple-element.137), channel_id=1, source_target_pairs={{0,8},{4,12},{8,16},{12,20},{16,24},{20,28},{24,0},{28,4},{1,9},{5... | collective-permute-start | bytes 786440 | tf_op jit(solution)/shard_map/ppermute | solution.py:325
  249.0 8.9 %arrange.4 = bf16[768,2048]{1,0:T(8,128)(2,1)} custom-call(bf16[2,768,1024]{2,1,0:T(8,128)(2,1)} %get-tuple-element.156.x_ref, bf16[2,1024,1024]{2,1,0:T(8,128)(2,1)} %copy-done.3), custom_call_target="tpu_custom_call" | custom-call | flops 1000 | bytes 6291456 | tf_op jit(solution)/shard_map/arrange/pallas_call | solution.py:251
  279.3 5.3 %collective-permute-done.17.refs_5_ = bf16[4,128,256]{2,1,0:T(8,128)(2,1)S(1)} collective-permute-done((bf16[4,128,256]{2,1,0:T(8,128)(2,1)}, bf16[4,128,256]{2,1,0:T(8,128)(2,1)S(1)}, u32[]{:S(2)}, u32[]{:S(2)}) %collective-permute-start.17) | collective-permute-done | bytes 262176 | tf_op jit(solution)/shard_map/ppermute | solution.py:325
  288.1 4.8 %project.5 = (bf16[2,512,1024]{2,1,0:T(8,128)(2,1)}, bf16[512,512]{1,0:T(8,128)(2,1)}) custom-call(s32[1]{0:T(128)} %bitcast.place_ref, bf16[2,1024,512]{2,1,0:T(8,128)(2,1)} %convolution_convert_fusion.weight_ref, bf16[4,128,256]{2,1,0:T(8,128)(2,1)} %get-tuple-element.158.refs_0_, bf16[4,128,256]{2,1,0:T(8,128)(2,1)} %collective-permute-done.13.refs_1_, ...), custom_call_target="tpu_custom_call" | custom-call | flops 1000 | bytes 4194304 | tf_op jit(solution)/shard_map/project/pallas_call | solution.py:218
  298.3 8.0 %collective-permute-done.34 = bf16[384,512]{1,0:T(8,128)(2,1)S(1)} collective-permute-done((bf16[384,512]{1,0:T(8,128)(2,1)S(1)}, bf16[384,512]{1,0:T(8,128)(2,1)S(1)}, u32[]{:S(2)}, u32[]{:S(2)}) %collective-permute-start.34) | collective-permute-done | bytes 393248 | tf_op jit(solution)/shard_map/ppermute | solution.py:331
  306.5 8.2 %collective-permute-done.40 = bf16[384,512]{1,0:T(8,128)(2,1)S(1)} collective-permute-done((bf16[384,512]{1,0:T(8,128)(2,1)S(1)}, bf16[384,512]{1,0:T(8,128)(2,1)S(1)}, u32[]{:S(2)}, u32[]{:S(2)}) %collective-permute-start.40) | collective-permute-done | bytes 393248 | tf_op jit(solution)/shard_map/ppermute | solution.py:331
  321.3 7.3 %last.3.refs_0_ = bf16[4,512,2048]{2,1,0:T(8,128)(2,1)} custom-call(bf16[4,192,512]{2,1,0:T(8,128)(2,1)} %bitcast.63, bf16[512,2048]{1,0:T(8,128)(2,1)} %slice_bitcast_fusion.up_ref, f32[1,2048]{1,0:T(1,128)} %get-tuple-element.173.bias_ref, bf16[4,192,2048]{2,1,0:T(8,128)(2,1)} %bitcast.61, bf16[4,192,2048]{2,1,0:T(8,128)(2,1)} %bitcast.66), custom_call_target="tpu_custom_call" | custom-call | flops 1000 | bytes 9437184 | tf_op jit(solution)/shard_map/last/pallas_call | solution.py:305
  329.7 7.3 %last.4.refs_0_ = bf16[4,512,2048]{2,1,0:T(8,128)(2,1)} custom-call(bf16[4,192,512]{2,1,0:T(8,128)(2,1)} %bitcast.64, bf16[512,2048]{1,0:T(8,128)(2,1)} %slice_bitcast_fusion.up_ref, f32[1,2048]{1,0:T(1,128)} %get-tuple-element.173.bias_ref, bf16[4,192,2048]{2,1,0:T(8,128)(2,1)} %bitcast.60, ...), custom_call_target="tpu_custom_call", output_to_operand_aliasing={{}: (5, {})} | custom-call | flops 1000 | bytes 9437184 | tf_op jit(solution)/shard_map/last/pallas_call | solution.py:305
  337.0 6.9 %arrange.5 = bf16[512,2048]{1,0:T(8,128)(2,1)} custom-call(bf16[2,512,1024]{2,1,0:T(8,128)(2,1)} %get-tuple-element.168.x_ref, bf16[2,1024,1024]{2,1,0:T(8,128)(2,1)} %copy-done.3), custom_call_target="tpu_custom_call" | custom-call | flops 1000 | bytes 4194304 | tf_op jit(solution)/shard_map/arrange/pallas_call | solution.py:251
  351.7 7.9 %collective-permute-done.46 = bf16[256,512]{1,0:T(8,128)(2,1)S(1)} collective-permute-done((bf16[256,512]{1,0:T(8,128)(2,1)S(1)}, bf16[256,512]{1,0:T(8,128)(2,1)S(1)}, u32[]{:S(2)}, u32[]{:S(2)}) %collective-permute-start.46) | collective-permute-done | bytes 262176 | tf_op jit(solution)/shard_map/ppermute | solution.py:331
  362.3 6.1 %last.5 = bf16[4,512,2048]{2,1,0:T(8,128)(2,1)} custom-call(bf16[4,128,512]{2,1,0:T(8,128)(2,1)} %bitcast.67, bf16[512,2048]{1,0:T(8,128)(2,1)} %slice_bitcast_fusion.up_ref, f32[1,2048]{1,0:T(1,128)} %get-tuple-element.173.bias_ref, bf16[4,128,2048]{2,1,0:T(8,128)(2,1)} %bitcast.62, bf16[4,128,2048]{2,1,0:T(8,128)(2,1)} %bitcast.69, ...), custom_call_target="tpu_custom_call", output_to_operand_aliasing={{}: (5, {})} | custom-call | flops 1000 | bytes 6291456 | tf_op jit(solution)/shard_map/last/pallas_call | solution.py:305
  (201 shorter events, 109.0 us)
Async XLA Ops:
  25.1 32.3 %collective-permute-start.3 = (bf16[4,192,256]{2,1,0:T(8,128)(2,1)}, bf16[4,192,256]{2,1,0:T(8,128)(2,1)S(1)}, u32[]{:S(2)}, u32[]{:S(2)}) collective-permute-start(bf16[4,192,256]{2,1,0:T(8,128)(2,1)} %get-tuple-element.89), channel_id=1, source_target_pairs={{0,4},{4,8},{8,12},{12,16},{16,20},{20,24},{24,28},{28,0},{1,5},{5... | collective-permute-start | bytes 1179656 | tf_op jit(solution)/shard_map/ppermute | solution.py:325
  28.1 51.7 %collective-permute-start.4 = (bf16[4,192,256]{2,1,0:T(8,128)(2,1)}, bf16[4,192,256]{2,1,0:T(8,128)(2,1)S(1)}, u32[]{:S(2)}, u32[]{:S(2)}) collective-permute-start(bf16[4,192,256]{2,1,0:T(8,128)(2,1)} %get-tuple-element.90), channel_id=1, source_target_pairs={{0,8},{4,12},{8,16},{12,20},{16,24},{20,28},{24,0},{28,4},{1,9},{5... | collective-permute-start | bytes 1179656 | tf_op jit(solution)/shard_map/ppermute | solution.py:325
  30.3 50.8 %collective-permute-start.5 = (bf16[4,192,256]{2,1,0:T(8,128)(2,1)}, bf16[4,192,256]{2,1,0:T(8,128)(2,1)}, u32[]{:S(2)}, u32[]{:S(2)}) collective-permute-start(bf16[4,192,256]{2,1,0:T(8,128)(2,1)} %get-tuple-element.91), channel_id=1, source_target_pairs={{0,12},{4,16},{8,20},{12,24},{16,28},{20,0},{24,4},{28,8},{1,13},{... | collective-permute-start | bytes 1179656 | tf_op jit(solution)/shard_map/ppermute | solution.py:325
  55.9 71.9 %collective-permute-start.10 = (bf16[8,192,256]{2,1,0:T(8,128)(2,1)}, bf16[8,192,256]{2,1,0:T(8,128)(2,1)S(1)}, u32[]{:S(2)}, u32[]{:S(2)}) collective-permute-start(bf16[8,192,256]{2,1,0:T(8,128)(2,1)} %bitcast.79), channel_id=1, source_target_pairs={{0,1},{1,2},{2,3},{3,0},{4,5},{5,6},{6,7},{7,4},{8,9},{9,10},{10,1... | collective-permute-start | bytes 2359304 | tf_op jit(solution)/shard_map/ppermute | solution.py:325
  55.9 72.0 %collective-permute-start.11 = (bf16[8,192,256]{2,1,0:T(8,128)(2,1)}, bf16[8,192,256]{2,1,0:T(8,128)(2,1)S(1)}, u32[]{:S(2)}, u32[]{:S(2)}) collective-permute-start(bf16[8,192,256]{2,1,0:T(8,128)(2,1)} %bitcast.78), channel_id=1, source_target_pairs={{0,2},{1,3},{2,0},{3,1},{4,6},{5,7},{6,4},{7,5},{8,10},{9,11},{10,... | collective-permute-start | bytes 2359304 | tf_op jit(solution)/shard_map/ppermute | solution.py:325
  57.4 71.9 %collective-permute-start.12 = (bf16[8,192,256]{2,1,0:T(8,128)(2,1)}, bf16[8,192,256]{2,1,0:T(8,128)(2,1)S(1)}, u32[]{:S(2)}, u32[]{:S(2)}) collective-permute-start(bf16[8,192,256]{2,1,0:T(8,128)(2,1)} %bitcast.77), channel_id=1, source_target_pairs={{0,3},{1,0},{2,1},{3,2},{4,7},{5,4},{6,5},{7,6},{8,11},{9,8},{10,9... | collective-permute-start | bytes 2359304 | tf_op jit(solution)/shard_map/ppermute | solution.py:325
  79.8 27.8 %collective-permute-start.6 = (bf16[4,192,256]{2,1,0:T(8,128)(2,1)}, bf16[4,192,256]{2,1,0:T(8,128)(2,1)S(1)}, u32[]{:S(2)}, u32[]{:S(2)}) collective-permute-start(bf16[4,192,256]{2,1,0:T(8,128)(2,1)} %get-tuple-element.92), channel_id=1, source_target_pairs={{0,16},{4,20},{8,24},{12,28},{16,0},{20,4},{24,8},{28,12},{1,17},{... | collective-permute-start | bytes 1179656 | tf_op jit(solution)/shard_map/ppermute | solution.py:325
  81.1 29.0 %collective-permute-start.7 = (bf16[4,192,256]{2,1,0:T(8,128)(2,1)}, bf16[4,192,256]{2,1,0:T(8,128)(2,1)S(1)}, u32[]{:S(2)}, u32[]{:S(2)}) collective-permute-start(bf16[4,192,256]{2,1,0:T(8,128)(2,1)} %get-tuple-element.93), channel_id=1, source_target_pairs={{0,20},{4,24},{8,28},{12,0},{16,4},{20,8},{24,12},{28,16},{1,21},{... | collective-permute-start | bytes 1179656 | tf_op jit(solution)/shard_map/ppermute | solution.py:325
  107.6 30.3 %collective-permute-start.8 = (bf16[4,192,256]{2,1,0:T(8,128)(2,1)}, bf16[4,192,256]{2,1,0:T(8,128)(2,1)}, u32[]{:S(2)}, u32[]{:S(2)}) collective-permute-start(bf16[4,192,256]{2,1,0:T(8,128)(2,1)} %get-tuple-element.94), channel_id=1, source_target_pairs={{0,24},{4,28},{8,0},{12,4},{16,8},{20,12},{24,16},{28,20},{1,25},{... | collective-permute-start | bytes 1179656 | tf_op jit(solution)/shard_map/ppermute | solution.py:325
  110.1 27.8 %collective-permute-start.9 = (bf16[4,192,256]{2,1,0:T(8,128)(2,1)}, bf16[4,192,256]{2,1,0:T(8,128)(2,1)}, u32[]{:S(2)}, u32[]{:S(2)}) collective-permute-start(bf16[4,192,256]{2,1,0:T(8,128)(2,1)} %get-tuple-element.95), channel_id=1, source_target_pairs={{0,28},{4,0},{8,4},{12,8},{16,12},{20,16},{24,20},{28,24},{1,29},{... | collective-permute-start | bytes 1179656 | tf_op jit(solution)/shard_map/ppermute | solution.py:325
  129.3 23.9 %collective-permute-start.2 = (bf16[8,128,256]{2,1,0:T(8,128)(2,1)}, bf16[8,128,256]{2,1,0:T(8,128)(2,1)}, u32[]{:S(2)}, u32[]{:S(2)}) collective-permute-start(bf16[8,128,256]{2,1,0:T(8,128)(2,1)} %bitcast.11), channel_id=1, source_target_pairs={{0,3},{1,0},{2,1},{3,2},{4,7},{5,4},{6,5},{7,6},{8,11},{9,8},{10,9... | collective-permute-start | bytes 1572872 | tf_op jit(solution)/shard_map/ppermute | solution.py:325
  141.6 28.1 %collective-permute-start.27 = (bf16[8,192,256]{2,1,0:T(8,128)(2,1)}, bf16[8,192,256]{2,1,0:T(8,128)(2,1)S(1)}, u32[]{:S(2)}, u32[]{:S(2)}) collective-permute-start(bf16[8,192,256]{2,1,0:T(8,128)(2,1)} %get-tuple-element.128), channel_id=1, source_target_pairs={{0,1},{1,2},{2,3},{3,0},{4,5},{5,6},{6,7},{7,4},{8,9},{9,10},{10,1... | collective-permute-start | bytes 2359304 | tf_op jit(solution)/shard_map/ppermute | solution.py:325
  141.6 29.5 %collective-permute-start.28 = (bf16[8,192,256]{2,1,0:T(8,128)(2,1)}, bf16[8,192,256]{2,1,0:T(8,128)(2,1)S(1)}, u32[]{:S(2)}, u32[]{:S(2)}) collective-permute-start(bf16[8,192,256]{2,1,0:T(8,128)(2,1)} %get-tuple-element.129), channel_id=1, source_target_pairs={{0,2},{1,3},{2,0},{3,1},{4,6},{5,7},{6,4},{7,5},{8,10},{9,11},{10,... | collective-permute-start | bytes 2359304 | tf_op jit(solution)/shard_map/ppermute | solution.py:325
  142.2 44.0 %collective-permute-start.29 = (bf16[8,192,256]{2,1,0:T(8,128)(2,1)}, bf16[8,192,256]{2,1,0:T(8,128)(2,1)S(1)}, u32[]{:S(2)}, u32[]{:S(2)}) collective-permute-start(bf16[8,192,256]{2,1,0:T(8,128)(2,1)} %get-tuple-element.130), channel_id=1, source_target_pairs={{0,3},{1,0},{2,1},{3,2},{4,7},{5,4},{6,5},{7,6},{8,11},{9,8},{10,9... | collective-permute-start | bytes 2359304 | tf_op jit(solution)/shard_map/ppermute | solution.py:325
  154.3 40.5 %collective-permute-start.22 = (bf16[4,192,256]{2,1,0:T(8,128)(2,1)}, bf16[4,192,256]{2,1,0:T(8,128)(2,1)}, u32[]{:S(2)}, u32[]{:S(2)}) collective-permute-start(bf16[4,192,256]{2,1,0:T(8,128)(2,1)} %get-tuple-element.114), channel_id=1, source_target_pairs={{0,12},{4,16},{8,20},{12,24},{16,28},{20,0},{24,4},{28,8},{1,13},{... | collective-permute-start | bytes 1179656 | tf_op jit(solution)/shard_map/ppermute | solution.py:325
  167.0 40.2 %collective-permute-start.23 = (bf16[4,192,256]{2,1,0:T(8,128)(2,1)}, bf16[4,192,256]{2,1,0:T(8,128)(2,1)S(1)}, u32[]{:S(2)}, u32[]{:S(2)}) collective-permute-start(bf16[4,192,256]{2,1,0:T(8,128)(2,1)} %get-tuple-element.115), channel_id=1, source_target_pairs={{0,16},{4,20},{8,24},{12,28},{16,0},{20,4},{24,8},{28,12},{1,17},{... | collective-permute-start | bytes 1179656 | tf_op jit(solution)/shard_map/ppermute | solution.py:325
  169.7 37.5 %collective-permute-start.24 = (bf16[4,192,256]{2,1,0:T(8,128)(2,1)}, bf16[4,192,256]{2,1,0:T(8,128)(2,1)}, u32[]{:S(2)}, u32[]{:S(2)}) collective-permute-start(bf16[4,192,256]{2,1,0:T(8,128)(2,1)} %get-tuple-element.116), channel_id=1, source_target_pairs={{0,20},{4,24},{8,28},{12,0},{16,4},{20,8},{24,12},{28,16},{1,21},{... | collective-permute-start | bytes 1179656 | tf_op jit(solution)/shard_map/ppermute | solution.py:325
  171.0 36.2 %collective-permute-start.25 = (bf16[4,192,256]{2,1,0:T(8,128)(2,1)}, bf16[4,192,256]{2,1,0:T(8,128)(2,1)}, u32[]{:S(2)}, u32[]{:S(2)}) collective-permute-start(bf16[4,192,256]{2,1,0:T(8,128)(2,1)} %get-tuple-element.117), channel_id=1, source_target_pairs={{0,24},{4,28},{8,0},{12,4},{16,8},{20,12},{24,16},{28,20},{1,25},{... | collective-permute-start | bytes 1179656 | tf_op jit(solution)/shard_map/ppermute | solution.py:325
  220.3 37.6 %collective-permute-start.31 = (bf16[384,512]{1,0:T(8,128)(2,1)S(1)}, bf16[384,512]{1,0:T(8,128)(2,1)}, u32[]{:S(2)}, u32[]{:S(2)}) collective-permute-start(bf16[384,512]{1,0:T(8,128)(2,1)S(1)} %add_convert_fusion.7), channel_id=1, source_target_pairs={{0,2},{1,3},{2,0},{3,1},{4,6},{5,7},{6,4},{7,5},{8,10},{9,11},{10,... | collective-permute-start | bytes 1179656 | tf_op jit(solution)/shard_map/ppermute | solution.py:331
  230.1 28.8 %collective-permute-start.38 = (bf16[384,512]{1,0:T(8,128)(2,1)S(1)}, bf16[384,512]{1,0:T(8,128)(2,1)}, u32[]{:S(2)}, u32[]{:S(2)}) collective-permute-start(bf16[384,512]{1,0:T(8,128)(2,1)S(1)} %add_convert_fusion.2), channel_id=1, source_target_pairs={{0,1},{1,0},{2,3},{3,2},{4,5},{5,4},{6,7},{7,6},{8,9},{9,8},{10,11... | collective-permute-start | bytes 1179656 | tf_op jit(solution)/shard_map/ppermute | solution.py:331
  230.8 40.1 %collective-permute-start.13 = (bf16[4,128,256]{2,1,0:T(8,128)(2,1)}, bf16[4,128,256]{2,1,0:T(8,128)(2,1)}, u32[]{:S(2)}, u32[]{:S(2)}) collective-permute-start(bf16[4,128,256]{2,1,0:T(8,128)(2,1)} %get-tuple-element.136), channel_id=1, source_target_pairs={{0,4},{4,8},{8,12},{12,16},{16,20},{20,24},{24,28},{28,0},{1,5},{5... | collective-permute-start | bytes 786440 | tf_op jit(solution)/shard_map/ppermute | solution.py:325
  236.5 36.9 %collective-permute-start.14 = (bf16[4,128,256]{2,1,0:T(8,128)(2,1)}, bf16[4,128,256]{2,1,0:T(8,128)(2,1)}, u32[]{:S(2)}, u32[]{:S(2)}) collective-permute-start(bf16[4,128,256]{2,1,0:T(8,128)(2,1)} %get-tuple-element.137), channel_id=1, source_target_pairs={{0,8},{4,12},{8,16},{12,20},{16,24},{20,28},{24,0},{28,4},{1,9},{5... | collective-permute-start | bytes 786440 | tf_op jit(solution)/shard_map/ppermute | solution.py:325
  249.0 25.8 %collective-permute-start.15 = (bf16[4,128,256]{2,1,0:T(8,128)(2,1)}, bf16[4,128,256]{2,1,0:T(8,128)(2,1)}, u32[]{:S(2)}, u32[]{:S(2)}) collective-permute-start(bf16[4,128,256]{2,1,0:T(8,128)(2,1)} %get-tuple-element.138), channel_id=1, source_target_pairs={{0,12},{4,16},{8,20},{12,24},{16,28},{20,0},{24,4},{28,8},{1,13},{... | collective-permute-start | bytes 786440 | tf_op jit(solution)/shard_map/ppermute | solution.py:325
  320.0 24.0 %collective-permute-start.44 = (bf16[256,512]{1,0:T(8,128)(2,1)S(1)}, bf16[256,512]{1,0:T(8,128)(2,1)S(1)}, u32[]{:S(2)}, u32[]{:S(2)}) collective-permute-start(bf16[256,512]{1,0:T(8,128)(2,1)S(1)} %add_convert_fusion.10), channel_id=1, source_target_pairs={{0,1},{1,0},{2,3},{3,2},{4,5},{5,4},{6,7},{7,6},{8,9},{9,8},{10,11... | collective-permute-start | bytes 786440 | tf_op jit(solution)/shard_map/ppermute | solution.py:331
  (55 other events, 678.3 us)
where the time goes:
time: 375 us; the launch traced here: 368 us
  Pallas kernels  137 us (37%)
  waiting for transfers between devices  114 us (30%)
  starting transfers between devices  78.1 us (21%)
  matrix products  18.3 us (5%)
  local copies, waits for them, and re-layouts  11.7 us (3%)
  other arithmetic  8.46 us (2%)
    ppermute x30, waiting for transfers between devices, spread(): moved.append(lax.ppermute(arrays[step], axis, pairs))  74.1 us
    ppermute x30, starting transfers between devices, spread(): moved.append(lax.ppermute(arrays[step], axis, pairs))  65.9 us
    pallas_call x3, Pallas kernels, gather(): pl.pallas_call(functools.partial(gather_kernel, by_owner), grid_spec=pltp...  64 us
    ppermute x18, waiting for transfers between devices, trade(): return lax.ppermute(value, axis, [(i, i ^ step) for i in range(size)])  39.7 us
    pallas_call x3, Pallas kernels, arrange(): pl.pallas_call(arrange_kernel, grid=(halves, rows // tile), in_specs=[pl....  24.5 us
    pallas_call x3, Pallas kernels, last(): pl.pallas_call(last_kernel, grid=(groups, part_rows // tile), in_specs=in...  20.7 us
    pallas_call x3, Pallas kernels, project(): pl.pallas_call(functools.partial(project_kernel, by_owner, min(256, rows)...  18 us
    ppermute x18, starting transfers between devices, trade(): return lax.ppermute(value, axis, [(i, i ^ step) for i in range(size)])  12.2 us
  transfers between devices with their start and end apart: 48, of which 18 were waited for; matrix products, arithmetic and copies ran while one was open for 8% of the time, Pallas kernels for 29%

commit v1 on v0

--- a/solution.py
+++ b/solution.py
@@ -257,7 +257,7 @@
         ],
         out_specs=pl.BlockSpec((tile, half_width), lambda h, i: (i, h)),
         out_shape=jax.ShapeDtypeStruct((rows, halves * half_width), x.dtype),
-        compiler_params=pltpu.CompilerParams(vmem_limit_bytes=60 * MIB),
+        compiler_params=pltpu.CompilerParams(vmem_limit_bytes=40 * MIB),
         cost_estimate=pl.CostEstimate(
             flops=1000,
             bytes_accessed=4 * rows * halves * half_width,
@@ -309,7 +309,7 @@
         out_specs=pl.BlockSpec((1, tile, width), lambda j, i: (j, start // tile + i, 0)),
         out_shape=jax.ShapeDtypeStruct(shape, jnp.bfloat16),
         input_output_aliases=aliases,
-        compiler_params=pltpu.CompilerParams(vmem_limit_bytes=60 * MIB),
+        compiler_params=pltpu.CompilerParams(vmem_limit_bytes=40 * MIB),
         cost_estimate=pl.CostEstimate(
             flops=1000, bytes_accessed=6 * rows * width, transcendentals=0
         ),
@@ -319,11 +319,11 @@
 
 def spread(arrays, axis):
     size = len(arrays)
-    moved = [arrays[0]]
-    for step in range(1, size):
+    moved = {0: arrays[0]}
+    for step in sorted(range(1, size), key=lambda step: abs(2 * step - size)):
         pairs = [(i, (i + step) % size) for i in range(size)]
-        moved.append(lax.ppermute(arrays[step], axis, pairs))
-    return moved
+        moved[step] = lax.ppermute(arrays[step], axis, pairs)
+    return [moved[step] for step in range(size)]
 
 
 def trade(value, axis, step):

time: 375 us -> 358 us (0.955)
  Pallas kernels: 137 us -> 115 us
  local copies, waits for them, and re-layouts: 11.7 us -> 26.5 us
  waiting for transfers between devices: 114 us -> 108 us
    unnamed x60 -> x98, local copies, waits for them, and re-layouts: 2.54 us -> 18.2 us
    pallas_call x3, Pallas kernels: 24.5 us -> 11.9 us  [arrange(): pl.pallas_call(arrange_kernel, grid=(halves, rows // tile), in_specs=[pl....]
    pallas_call x3, Pallas kernels: 20.7 us -> 10.9 us  [last(): pl.pallas_call(last_kernel, grid=(groups, part_rows // tile), in_specs=in...]
    ppermute x30, waiting for transfers between devices: 74.1 us -> 69.7 us  [spread(): moved[step] = lax.ppermute(arrays[step], axis, pairs)]
  transfers between devices with their start and end apart: 48 -> 48, of which waited for: 18 -> 17; matrix products, arithmetic and copies ran while one was open for 8% -> 8% of each run, Pallas kernels for 29% -> 25%
where the time goes in v1:
time: 358 us; the launch traced here: 352 us
  Pallas kernels  115 us (32%)
  waiting for transfers between devices  108 us (30%)
  starting transfers between devices  77.7 us (22%)
  local copies, waits for them, and re-layouts  26.5 us (7%)
  matrix products  15.6 us (4%)
  other arithmetic  8.94 us (2%)
    ppermute x30, waiting for transfers between devices, spread(): moved[step] = lax.ppermute(arrays[step], axis, pairs)  69.7 us
    ppermute x30, starting transfers between devices, spread(): moved[step] = lax.ppermute(arrays[step], axis, pairs)  65 us
    pallas_call x3, Pallas kernels, gather(): pl.pallas_call(functools.partial(gather_kernel, by_owner), grid_spec=pltp...  64.1 us
    ppermute x18, waiting for transfers between devices, trade(): return lax.ppermute(value, axis, [(i, i ^ step) for i in range(size)])  37.9 us
    unnamed x98, local copies, waits for them, and re-layouts  18.2 us
    pallas_call x3, Pallas kernels, project(): pl.pallas_call(functools.partial(project_kernel, by_owner, min(256, rows)...  18 us
    ppermute x18, starting transfers between devices, trade(): return lax.ppermute(value, axis, [(i, i ^ step) for i in range(size)])  12.7 us
    pallas_call x3, Pallas kernels, arrange(): pl.pallas_call(arrange_kernel, grid=(halves, rows // tile), in_specs=[pl....  11.9 us
  transfers between devices with their start and end apart: 48, of which 17 were waited for; matrix products, arithmetic and copies ran while one was open for 8% of the time, Pallas kernels for 25%

profile of v1, /device:TPU:0, one launch (start us, length us, event | category | flops | bytes accessed | tf_op | source)
XLA Modules:
  0.0 352.0 jit_solution(365503238913610893)
XLA Ops:
  2.0 23.1 %gather.9 = (bf16[4,192,256]{2,1,0:T(8,128)(2,1)}, bf16[4,192,256]{2,1,0:T(8,128)(2,1)}, bf16[4,192,256]{2,1,0:T(8,128)(2,1)}, bf16[4,192,256]{2,1,0:T(8,128)(2,...) custom-call(s32[1]{0:T(128)} %bitcast.place_ref, ...), custom_call_target="tpu_custom_call" | custom-call | flops 1000 | bytes 16777216 | tf_op jit(solution)/shard_map/gather/pallas_call | solution.py:114
  33.0 23.0 %gather.10 = (bf16[1536,256]{1,0:T(8,128)(2,1)}, bf16[1536,256]{1,0:T(8,128)(2,1)}, bf16[1536,256]{1,0:T(8,128)(2,1)}, bf16[1536,256]{1,0:T(8,128)(2,1)}) custom-call(s32[1]{0:T(128)} %bitcast.place_ref, s32[8,1,1536]{2,1,0:T(1,128)} %reshape.157.idx_ref, bf16[8,8192,128]{2,1,0:T(8,128)(2,1)} %table_ref.5), custom_call_target="tpu_custom_call" | custom-call | flops 1000 | bytes 16777216 | tf_op jit(solution)/shard_map/gather/pallas_call | solution.py:114
  60.4 18.0 %gather.11 = (bf16[1024,256]{1,0:T(8,128)(2,1)}, bf16[1024,256]{1,0:T(8,128)(2,1)}, bf16[1024,256]{1,0:T(8,128)(2,1)}, bf16[1024,256]{1,0:T(8,128)(2,1)}) custom-call(s32[1]{0:T(128)} %bitcast.place_ref, s32[8,1,1024]{2,1,0:T(1,128)} %bitcast.73, bf16[8,8192,128]{2,1,0:T(8,128)(2,1)} %table_ref.5), custom_call_target="tpu_custom_call" | custom-call | flops 1000 | bytes 16777216 | tf_op jit(solution)/shard_map/gather/pallas_call | solution.py:114
  85.4 23.0 %collective-permute-done.6.refs_4_ = bf16[4,192,256]{2,1,0:T(8,128)(2,1)S(1)} collective-permute-done((bf16[4,192,256]{2,1,0:T(8,128)(2,1)}, bf16[4,192,256]{2,1,0:T(8,128)(2,1)S(1)}, u32[]{:S(2)}, u32[]{:S(2)}) %collective-permute-start.6) | collective-permute-done | bytes 393248 | tf_op jit(solution)/shard_map/ppermute | solution.py:325
  110.9 17.7 %collective-permute-start.9 = (bf16[4,192,256]{2,1,0:T(8,128)(2,1)}, bf16[4,192,256]{2,1,0:T(8,128)(2,1)}, u32[]{:S(2)}, u32[]{:S(2)}) collective-permute-start(bf16[4,192,256]{2,1,0:T(8,128)(2,1)} %get-tuple-element.95), channel_id=1, source_target_pairs={{0,28},{4,0},{8,4},{12,8},{16,12},{20,16},{24,20},{28,24},{1,29},{... | collective-permute-start | bytes 1179656 | tf_op jit(solution)/shard_map/ppermute | solution.py:325
  146.6 7.3 %collective-permute-done.2.refs_3_ = bf16[8,128,256]{2,1,0:T(8,128)(2,1)} collective-permute-done((bf16[8,128,256]{2,1,0:T(8,128)(2,1)}, bf16[8,128,256]{2,1,0:T(8,128)(2,1)}, u32[]{:S(2)}, u32[]{:S(2)}) %collective-permute-start.2) | collective-permute-done | bytes 524320 | tf_op jit(solution)/shard_map/ppermute | solution.py:325
  160.1 7.6 %collective-permute-done.21.refs_2_ = bf16[4,192,256]{2,1,0:T(8,128)(2,1)} collective-permute-done((bf16[4,192,256]{2,1,0:T(8,128)(2,1)}, bf16[4,192,256]{2,1,0:T(8,128)(2,1)}, u32[]{:S(2)}, u32[]{:S(2)}) %collective-permute-start.21) | collective-permute-done | bytes 393248 | tf_op jit(solution)/shard_map/ppermute | solution.py:325
  171.7 15.2 %collective-permute-done.29.refs_3_ = bf16[8,192,256]{2,1,0:T(8,128)(2,1)S(1)} collective-permute-done((bf16[8,192,256]{2,1,0:T(8,128)(2,1)}, bf16[8,192,256]{2,1,0:T(8,128)(2,1)S(1)}, u32[]{:S(2)}, u32[]{:S(2)}) %collective-permute-start.29) | collective-permute-done | bytes 786464 | tf_op jit(solution)/shard_map/ppermute | solution.py:325
  187.8 6.6 %project.3 = (bf16[2,768,1024]{2,1,0:T(8,128)(2,1)}, bf16[768,512]{1,0:T(8,128)(2,1)}) custom-call(s32[1]{0:T(128)} %bitcast.place_ref, bf16[2,1024,512]{2,1,0:T(8,128)(2,1)} %convolution_convert_fusion.weight_ref, bf16[8,192,256]{2,1,0:T(8,128)(2,1)} %get-tuple-element.143.refs_0_, bf16[8,192,256]{2,1,0:T(8,128)(2,1)} %copy-done.29, ...), custom_call_target="tpu_custom_call" | custom-call | flops 1000 | bytes 6291456 | tf_op jit(solution)/shard_map/project/pallas_call | solution.py:218
  195.4 4.3 %collective-permute-start.36 = (bf16[384,512]{1,0:T(8,128)(2,1)S(1)}, bf16[384,512]{1,0:T(8,128)(2,1)S(1)}, u32[]{:S(2)}, u32[]{:S(2)}) collective-permute-start(bf16[384,512]{1,0:T(8,128)(2,1)S(1)} %constant_dynamic-slice_fusion.3), channel_id=1, source_target_pairs={{0,1},{1,0},{2,3},{3,2},{4,5},{5,4},{6,7},{7,6},{8,9},{9,8},{10,11... | collective-permute-start | bytes 1179656 | tf_op jit(solution)/shard_map/ppermute | solution.py:331
  203.8 4.4 %arrange.3 = bf16[768,2048]{1,0:T(8,128)(2,1)S(1)} custom-call(bf16[2,768,1024]{2,1,0:T(8,128)(2,1)S(1)} %copy-done.12, bf16[2,1024,1024]{2,1,0:T(8,128)(2,1)S(1)} %copy-done.3), custom_call_target="tpu_custom_call" | custom-call | flops 1000 | bytes 6291456 | tf_op jit(solution)/shard_map/arrange/pallas_call | solution.py:251
  211.0 6.6 %project.4 = (bf16[2,768,1024]{2,1,0:T(8,128)(2,1)}, bf16[768,512]{1,0:T(8,128)(2,1)}) custom-call(s32[1]{0:T(128)} %bitcast.place_ref, bf16[2,1024,512]{2,1,0:T(8,128)(2,1)} %convolution_convert_fusion.weight_ref, bf16[4,192,256]{2,1,0:T(8,128)(2,1)} %get-tuple-element.148.refs_0_, bf16[4,192,256]{2,1,0:T(8,128)(2,1)} %collective-permute-done.20.refs_1_, ...), custom_call_target="tpu_custom_call" | custom-call | flops 1000 | bytes 6291456 | tf_op jit(solution)/shard_map/project/pallas_call | solution.py:218
  223.4 7.6 %collective-permute-done.37 = bf16[384,512]{1,0:T(8,128)(2,1)S(1)} collective-permute-done((bf16[384,512]{1,0:T(8,128)(2,1)S(1)}, bf16[384,512]{1,0:T(8,128)(2,1)S(1)}, u32[]{:S(2)}, u32[]{:S(2)}) %collective-permute-start.37) | collective-permute-done | bytes 393248 | tf_op jit(solution)/shard_map/ppermute | solution.py:331
  231.9 5.1 %collective-permute-start.13 = (bf16[4,128,256]{2,1,0:T(8,128)(2,1)}, bf16[4,128,256]{2,1,0:T(8,128)(2,1)S(1)}, u32[]{:S(2)}, u32[]{:S(2)}) collective-permute-start(bf16[4,128,256]{2,1,0:T(8,128)(2,1)} %get-tuple-element.136), channel_id=1, source_target_pairs={{0,4},{4,8},{8,12},{12,16},{16,20},{20,24},{24,28},{28,0},{1,5},{5... | collective-permute-start | bytes 786440 | tf_op jit(solution)/shard_map/ppermute | solution.py:325
  237.0 12.8 %collective-permute-start.14 = (bf16[4,128,256]{2,1,0:T(8,128)(2,1)}, bf16[4,128,256]{2,1,0:T(8,128)(2,1)S(1)}, u32[]{:S(2)}, u32[]{:S(2)}) collective-permute-start(bf16[4,128,256]{2,1,0:T(8,128)(2,1)} %get-tuple-element.137), channel_id=1, source_target_pairs={{0,8},{4,12},{8,16},{12,20},{16,24},{20,28},{24,0},{28,4},{1,9},{5... | collective-permute-start | bytes 786440 | tf_op jit(solution)/shard_map/ppermute | solution.py:325
  253.9 4.4 %arrange.4 = bf16[768,2048]{1,0:T(8,128)(2,1)S(1)} custom-call(bf16[2,768,1024]{2,1,0:T(8,128)(2,1)S(1)} %copy-done.11, bf16[2,1024,1024]{2,1,0:T(8,128)(2,1)S(1)} %copy-done.4), custom_call_target="tpu_custom_call" | custom-call | flops 1000 | bytes 6291456 | tf_op jit(solution)/shard_map/arrange/pallas_call | solution.py:251
  263.2 3.9 %collective-permute-start.17 = (bf16[4,128,256]{2,1,0:T(8,128)(2,1)}, bf16[4,128,256]{2,1,0:T(8,128)(2,1)}, u32[]{:S(2)}, u32[]{:S(2)}) collective-permute-start(bf16[4,128,256]{2,1,0:T(8,128)(2,1)} %get-tuple-element.140), channel_id=1, source_target_pairs={{0,20},{4,24},{8,28},{12,0},{16,4},{20,8},{24,12},{28,16},{1,21},{... | collective-permute-start | bytes 786440 | tf_op jit(solution)/shard_map/ppermute | solution.py:325
  280.3 5.4 %collective-permute-done.17.refs_5_ = bf16[4,128,256]{2,1,0:T(8,128)(2,1)} collective-permute-done((bf16[4,128,256]{2,1,0:T(8,128)(2,1)}, bf16[4,128,256]{2,1,0:T(8,128)(2,1)}, u32[]{:S(2)}, u32[]{:S(2)}) %collective-permute-start.17) | collective-permute-done | bytes 262176 | tf_op jit(solution)/shard_map/ppermute | solution.py:325
  288.6 4.9 %project.5 = (bf16[2,512,1024]{2,1,0:T(8,128)(2,1)}, bf16[512,512]{1,0:T(8,128)(2,1)}) custom-call(s32[1]{0:T(128)} %bitcast.place_ref, bf16[2,1024,512]{2,1,0:T(8,128)(2,1)} %convolution_convert_fusion.weight_ref, bf16[4,128,256]{2,1,0:T(8,128)(2,1)} %get-tuple-element.158.refs_0_, bf16[4,128,256]{2,1,0:T(8,128)(2,1)} %copy-done.42, ...), custom_call_target="tpu_custom_call" | custom-call | flops 1000 | bytes 4194304 | tf_op jit(solution)/shard_map/project/pallas_call | solution.py:218
  301.2 6.9 %collective-permute-done.34 = bf16[384,512]{1,0:T(8,128)(2,1)S(1)} collective-permute-done((bf16[384,512]{1,0:T(8,128)(2,1)S(1)}, bf16[384,512]{1,0:T(8,128)(2,1)S(1)}, u32[]{:S(2)}, u32[]{:S(2)}) %collective-permute-start.34) | collective-permute-done | bytes 393248 | tf_op jit(solution)/shard_map/ppermute | solution.py:331
  308.2 8.2 %collective-permute-done.40 = bf16[384,512]{1,0:T(8,128)(2,1)S(1)} collective-permute-done((bf16[384,512]{1,0:T(8,128)(2,1)S(1)}, bf16[384,512]{1,0:T(8,128)(2,1)S(1)}, u32[]{:S(2)}, u32[]{:S(2)}) %collective-permute-start.40) | collective-permute-done | bytes 393248 | tf_op jit(solution)/shard_map/ppermute | solution.py:331
  316.9 4.6 %collective-permute-done.43 = bf16[256,512]{1,0:T(8,128)(2,1)S(1)} collective-permute-done((bf16[256,512]{1,0:T(8,128)(2,1)S(1)}, bf16[256,512]{1,0:T(8,128)(2,1)S(1)}, u32[]{:S(2)}, u32[]{:S(2)}) %collective-permute-start.43) | collective-permute-done | bytes 262176 | tf_op jit(solution)/shard_map/ppermute | solution.py:331
  326.2 3.8 %last.4.refs_0_ = bf16[4,512,2048]{2,1,0:T(8,128)(2,1)} custom-call(bf16[4,192,512]{2,1,0:T(8,128)(2,1)S(1)} %bitcast.64, bf16[512,2048]{1,0:T(8,128)(2,1)S(1)} %slice_bitcast_fusion.up_ref, f32[1,2048]{1,0:T(1,128)S(1)} %get-tuple-element.173.bias_ref, bf16[4,192,2048]{2,1,0:T(8,128)(2,1)S(1)} %bitcast.60, ...), custom_call_target="tpu_custom_call", output_to_operand_aliasing={{}: (5, {})} | custom-call | flops 1000 | bytes 9437184 | tf_op jit(solution)/shard_map/last/pallas_call | solution.py:305
  339.1 7.9 %collective-permute-done.46 = bf16[256,512]{1,0:T(8,128)(2,1)S(1)} collective-permute-done((bf16[256,512]{1,0:T(8,128)(2,1)S(1)}, bf16[256,512]{1,0:T(8,128)(2,1)S(1)}, u32[]{:S(2)}, u32[]{:S(2)}) %collective-permute-start.46) | collective-permute-done | bytes 262176 | tf_op jit(solution)/shard_map/ppermute | solution.py:331
  (239 shorter events, 119.0 us)
Async XLA Ops:
  25.1 32.3 %collective-permute-start.3 = (bf16[4,192,256]{2,1,0:T(8,128)(2,1)}, bf16[4,192,256]{2,1,0:T(8,128)(2,1)S(1)}, u32[]{:S(2)}, u32[]{:S(2)}) collective-permute-start(bf16[4,192,256]{2,1,0:T(8,128)(2,1)} %get-tuple-element.89), channel_id=1, source_target_pairs={{0,4},{4,8},{8,12},{12,16},{16,20},{20,24},{24,28},{28,0},{1,5},{5... | collective-permute-start | bytes 1179656 | tf_op jit(solution)/shard_map/ppermute | solution.py:325
  28.1 52.4 %collective-permute-start.4 = (bf16[4,192,256]{2,1,0:T(8,128)(2,1)}, bf16[4,192,256]{2,1,0:T(8,128)(2,1)S(1)}, u32[]{:S(2)}, u32[]{:S(2)}) collective-permute-start(bf16[4,192,256]{2,1,0:T(8,128)(2,1)} %get-tuple-element.90), channel_id=1, source_target_pairs={{0,8},{4,12},{8,16},{12,20},{16,24},{20,28},{24,0},{28,4},{1,9},{5... | collective-permute-start | bytes 1179656 | tf_op jit(solution)/shard_map/ppermute | solution.py:325
  30.4 51.4 %collective-permute-start.5 = (bf16[4,192,256]{2,1,0:T(8,128)(2,1)}, bf16[4,192,256]{2,1,0:T(8,128)(2,1)S(1)}, u32[]{:S(2)}, u32[]{:S(2)}) collective-permute-start(bf16[4,192,256]{2,1,0:T(8,128)(2,1)} %get-tuple-element.91), channel_id=1, source_target_pairs={{0,12},{4,16},{8,20},{12,24},{16,28},{20,0},{24,4},{28,8},{1,13},{... | collective-permute-start | bytes 1179656 | tf_op jit(solution)/shard_map/ppermute | solution.py:325
  55.9 72.6 %collective-permute-start.10 = (bf16[8,192,256]{2,1,0:T(8,128)(2,1)}, bf16[8,192,256]{2,1,0:T(8,128)(2,1)S(1)}, u32[]{:S(2)}, u32[]{:S(2)}) collective-permute-start(bf16[8,192,256]{2,1,0:T(8,128)(2,1)} %bitcast.79), channel_id=1, source_target_pairs={{0,1},{1,2},{2,3},{3,0},{4,5},{5,6},{6,7},{7,4},{8,9},{9,10},{10,1... | collective-permute-start | bytes 2359304 | tf_op jit(solution)/shard_map/ppermute | solution.py:325
  55.9 72.6 %collective-permute-start.11 = (bf16[8,192,256]{2,1,0:T(8,128)(2,1)}, bf16[8,192,256]{2,1,0:T(8,128)(2,1)S(1)}, u32[]{:S(2)}, u32[]{:S(2)}) collective-permute-start(bf16[8,192,256]{2,1,0:T(8,128)(2,1)} %bitcast.78), channel_id=1, source_target_pairs={{0,2},{1,3},{2,0},{3,1},{4,6},{5,7},{6,4},{7,5},{8,10},{9,11},{10,... | collective-permute-start | bytes 2359304 | tf_op jit(solution)/shard_map/ppermute | solution.py:325
  58.2 71.8 %collective-permute-start.12 = (bf16[8,192,256]{2,1,0:T(8,128)(2,1)}, bf16[8,192,256]{2,1,0:T(8,128)(2,1)S(1)}, u32[]{:S(2)}, u32[]{:S(2)}) collective-permute-start(bf16[8,192,256]{2,1,0:T(8,128)(2,1)} %bitcast.77), channel_id=1, source_target_pairs={{0,3},{1,0},{2,1},{3,2},{4,7},{5,4},{6,5},{7,6},{8,11},{9,8},{10,9... | collective-permute-start | bytes 2359304 | tf_op jit(solution)/shard_map/ppermute | solution.py:325
  80.6 27.8 %collective-permute-start.6 = (bf16[4,192,256]{2,1,0:T(8,128)(2,1)}, bf16[4,192,256]{2,1,0:T(8,128)(2,1)S(1)}, u32[]{:S(2)}, u32[]{:S(2)}) collective-permute-start(bf16[4,192,256]{2,1,0:T(8,128)(2,1)} %get-tuple-element.92), channel_id=1, source_target_pairs={{0,16},{4,20},{8,24},{12,28},{16,0},{20,4},{24,8},{28,12},{1,17},{... | collective-permute-start | bytes 1179656 | tf_op jit(solution)/shard_map/ppermute | solution.py:325
  81.9 29.0 %collective-permute-start.7 = (bf16[4,192,256]{2,1,0:T(8,128)(2,1)}, bf16[4,192,256]{2,1,0:T(8,128)(2,1)S(1)}, u32[]{:S(2)}, u32[]{:S(2)}) collective-permute-start(bf16[4,192,256]{2,1,0:T(8,128)(2,1)} %get-tuple-element.93), channel_id=1, source_target_pairs={{0,20},{4,24},{8,28},{12,0},{16,4},{20,8},{24,12},{28,16},{1,21},{... | collective-permute-start | bytes 1179656 | tf_op jit(solution)/shard_map/ppermute | solution.py:325
  108.4 32.3 %collective-permute-start.8 = (bf16[4,192,256]{2,1,0:T(8,128)(2,1)}, bf16[4,192,256]{2,1,0:T(8,128)(2,1)}, u32[]{:S(2)}, u32[]{:S(2)}) collective-permute-start(bf16[4,192,256]{2,1,0:T(8,128)(2,1)} %get-tuple-element.94), channel_id=1, source_target_pairs={{0,24},{4,28},{8,0},{12,4},{16,8},{20,12},{24,16},{28,20},{1,25},{... | collective-permute-start | bytes 1179656 | tf_op jit(solution)/shard_map/ppermute | solution.py:325
  110.9 29.9 %collective-permute-start.9 = (bf16[4,192,256]{2,1,0:T(8,128)(2,1)}, bf16[4,192,256]{2,1,0:T(8,128)(2,1)}, u32[]{:S(2)}, u32[]{:S(2)}) collective-permute-start(bf16[4,192,256]{2,1,0:T(8,128)(2,1)} %get-tuple-element.95), channel_id=1, source_target_pairs={{0,28},{4,0},{8,4},{12,8},{16,12},{20,16},{24,20},{28,24},{1,29},{... | collective-permute-start | bytes 1179656 | tf_op jit(solution)/shard_map/ppermute | solution.py:325
  130.0 23.9 %collective-permute-start.2 = (bf16[8,128,256]{2,1,0:T(8,128)(2,1)}, bf16[8,128,256]{2,1,0:T(8,128)(2,1)}, u32[]{:S(2)}, u32[]{:S(2)}) collective-permute-start(bf16[8,128,256]{2,1,0:T(8,128)(2,1)} %bitcast.11), channel_id=1, source_target_pairs={{0,3},{1,0},{2,1},{3,2},{4,7},{5,4},{6,5},{7,6},{8,11},{9,8},{10,9... | collective-permute-start | bytes 1572872 | tf_op jit(solution)/shard_map/ppermute | solution.py:325
  144.4 26.1 %collective-permute-start.27 = (bf16[8,192,256]{2,1,0:T(8,128)(2,1)}, bf16[8,192,256]{2,1,0:T(8,128)(2,1)S(1)}, u32[]{:S(2)}, u32[]{:S(2)}) collective-permute-start(bf16[8,192,256]{2,1,0:T(8,128)(2,1)} %get-tuple-element.128), channel_id=1, source_target_pairs={{0,1},{1,2},{2,3},{3,0},{4,5},{5,6},{6,7},{7,4},{8,9},{9,10},{10,1... | collective-permute-start | bytes 2359304 | tf_op jit(solution)/shard_map/ppermute | solution.py:325
  144.4 27.4 %collective-permute-start.28 = (bf16[8,192,256]{2,1,0:T(8,128)(2,1)}, bf16[8,192,256]{2,1,0:T(8,128)(2,1)S(1)}, u32[]{:S(2)}, u32[]{:S(2)}) collective-permute-start(bf16[8,192,256]{2,1,0:T(8,128)(2,1)} %get-tuple-element.129), channel_id=1, source_target_pairs={{0,2},{1,3},{2,0},{3,1},{4,6},{5,7},{6,4},{7,5},{8,10},{9,11},{10,... | collective-permute-start | bytes 2359304 | tf_op jit(solution)/shard_map/ppermute | solution.py:325
  145.0 41.9 %collective-permute-start.29 = (bf16[8,192,256]{2,1,0:T(8,128)(2,1)}, bf16[8,192,256]{2,1,0:T(8,128)(2,1)S(1)}, u32[]{:S(2)}, u32[]{:S(2)}) collective-permute-start(bf16[8,192,256]{2,1,0:T(8,128)(2,1)} %get-tuple-element.130), channel_id=1, source_target_pairs={{0,3},{1,0},{2,1},{3,2},{4,7},{5,4},{6,5},{7,6},{8,11},{9,8},{10,9... | collective-permute-start | bytes 2359304 | tf_op jit(solution)/shard_map/ppermute | solution.py:325
  157.1 38.3 %collective-permute-start.22 = (bf16[4,192,256]{2,1,0:T(8,128)(2,1)}, bf16[4,192,256]{2,1,0:T(8,128)(2,1)}, u32[]{:S(2)}, u32[]{:S(2)}) collective-permute-start(bf16[4,192,256]{2,1,0:T(8,128)(2,1)} %get-tuple-element.114), channel_id=1, source_target_pairs={{0,12},{4,16},{8,20},{12,24},{16,28},{20,0},{24,4},{28,8},{1,13},{... | collective-permute-start | bytes 1179656 | tf_op jit(solution)/shard_map/ppermute | solution.py:325
  167.7 42.3 %collective-permute-start.23 = (bf16[4,192,256]{2,1,0:T(8,128)(2,1)}, bf16[4,192,256]{2,1,0:T(8,128)(2,1)S(1)}, u32[]{:S(2)}, u32[]{:S(2)}) collective-permute-start(bf16[4,192,256]{2,1,0:T(8,128)(2,1)} %get-tuple-element.115), channel_id=1, source_target_pairs={{0,16},{4,20},{8,24},{12,28},{16,0},{20,4},{24,8},{28,12},{1,17},{... | collective-permute-start | bytes 1179656 | tf_op jit(solution)/shard_map/ppermute | solution.py:325
  170.4 39.6 %collective-permute-start.24 = (bf16[4,192,256]{2,1,0:T(8,128)(2,1)}, bf16[4,192,256]{2,1,0:T(8,128)(2,1)S(1)}, u32[]{:S(2)}, u32[]{:S(2)}) collective-permute-start(bf16[4,192,256]{2,1,0:T(8,128)(2,1)} %get-tuple-element.116), channel_id=1, source_target_pairs={{0,20},{4,24},{8,28},{12,0},{16,4},{20,8},{24,12},{28,16},{1,21},{... | collective-permute-start | bytes 1179656 | tf_op jit(solution)/shard_map/ppermute | solution.py:325
  171.7 38.3 %collective-permute-start.25 = (bf16[4,192,256]{2,1,0:T(8,128)(2,1)}, bf16[4,192,256]{2,1,0:T(8,128)(2,1)S(1)}, u32[]{:S(2)}, u32[]{:S(2)}) collective-permute-start(bf16[4,192,256]{2,1,0:T(8,128)(2,1)} %get-tuple-element.117), channel_id=1, source_target_pairs={{0,24},{4,28},{8,0},{12,4},{16,8},{20,12},{24,16},{28,20},{1,25},{... | collective-permute-start | bytes 1179656 | tf_op jit(solution)/shard_map/ppermute | solution.py:325
  195.4 23.5 %collective-permute-start.36 = (bf16[384,512]{1,0:T(8,128)(2,1)S(1)}, bf16[384,512]{1,0:T(8,128)(2,1)S(1)}, u32[]{:S(2)}, u32[]{:S(2)}) collective-permute-start(bf16[384,512]{1,0:T(8,128)(2,1)S(1)} %constant_dynamic-slice_fusion.3), channel_id=1, source_target_pairs={{0,1},{1,0},{2,3},{3,2},{4,5},{5,4},{6,7},{7,6},{8,9},{9,8},{10,11... | collective-permute-start | bytes 1179656 | tf_op jit(solution)/shard_map/ppermute | solution.py:331
  221.9 36.5 %collective-permute-start.31 = (bf16[384,512]{1,0:T(8,128)(2,1)S(1)}, bf16[384,512]{1,0:T(8,128)(2,1)}, u32[]{:S(2)}, u32[]{:S(2)}) collective-permute-start(bf16[384,512]{1,0:T(8,128)(2,1)S(1)} %add_convert_fusion.7), channel_id=1, source_target_pairs={{0,2},{1,3},{2,0},{3,1},{4,6},{5,7},{6,4},{7,5},{8,10},{9,11},{10,... | collective-permute-start | bytes 1179656 | tf_op jit(solution)/shard_map/ppermute | solution.py:331
  231.9 27.7 %collective-permute-start.38 = (bf16[384,512]{1,0:T(8,128)(2,1)}, bf16[384,512]{1,0:T(8,128)(2,1)}, u32[]{:S(2)}, u32[]{:S(2)}) collective-permute-start(bf16[384,512]{1,0:T(8,128)(2,1)} %add_convert_fusion.2), channel_id=1, source_target_pairs={{0,1},{1,0},{2,3},{3,2},{4,5},{5,4},{6,7},{7,6},{8,9},{9,8},{10,11... | collective-permute-start | bytes 1179656 | tf_op jit(solution)/shard_map/ppermute | solution.py:331
  231.9 39.1 %collective-permute-start.13 = (bf16[4,128,256]{2,1,0:T(8,128)(2,1)}, bf16[4,128,256]{2,1,0:T(8,128)(2,1)S(1)}, u32[]{:S(2)}, u32[]{:S(2)}) collective-permute-start(bf16[4,128,256]{2,1,0:T(8,128)(2,1)} %get-tuple-element.136), channel_id=1, source_target_pairs={{0,4},{4,8},{8,12},{12,16},{16,20},{20,24},{24,28},{28,0},{1,5},{5... | collective-permute-start | bytes 786440 | tf_op jit(solution)/shard_map/ppermute | solution.py:325
  237.0 36.5 %collective-permute-start.14 = (bf16[4,128,256]{2,1,0:T(8,128)(2,1)}, bf16[4,128,256]{2,1,0:T(8,128)(2,1)S(1)}, u32[]{:S(2)}, u32[]{:S(2)}) collective-permute-start(bf16[4,128,256]{2,1,0:T(8,128)(2,1)} %get-tuple-element.137), channel_id=1, source_target_pairs={{0,8},{4,12},{8,16},{12,20},{16,24},{20,28},{24,0},{28,4},{1,9},{5... | collective-permute-start | bytes 786440 | tf_op jit(solution)/shard_map/ppermute | solution.py:325
  249.8 25.2 %collective-permute-start.15 = (bf16[4,128,256]{2,1,0:T(8,128)(2,1)}, bf16[4,128,256]{2,1,0:T(8,128)(2,1)S(1)}, u32[]{:S(2)}, u32[]{:S(2)}) collective-permute-start(bf16[4,128,256]{2,1,0:T(8,128)(2,1)} %get-tuple-element.138), channel_id=1, source_target_pairs={{0,12},{4,16},{8,20},{12,24},{16,28},{20,0},{24,4},{28,8},{1,13},{... | collective-permute-start | bytes 786440 | tf_op jit(solution)/shard_map/ppermute | solution.py:325
  (74 other events, 647.5 us)

commit v2 on v1

--- a/solution.py
+++ b/solution.py
@@ -1,4 +1,5 @@
 import functools
+import math
 
 import jax
 import jax.numpy as jnp
@@ -8,8 +9,8 @@
 from jax.sharding import PartitionSpec as P
 
 
-PLAN = ((3, True), (3, False), (2, False))
-UNROLL = 32
+PLAN = ((3, True), (2, False), (3, False))
+UNROLL = 64
 WIDEN = 1024
 MIX = 32
 MIB = 2**20
@@ -278,8 +279,8 @@
     groups, _, width = shape
     part_rows = low.shape[0] // groups
     rank = low.shape[1]
-    tile = part_rows
-    while start % tile or tile > 256:
+    tile = math.gcd(part_rows, start)
+    while tile > 256:
         tile //= 2
     row_spec = lambda size: pl.BlockSpec((1, tile, size), lambda j, i: (j, i, 0))
     operands = [
@@ -378,11 +379,11 @@
     )
 
     unit = share // sum(size for size, _ in PLAN)
-    starts, sizes, at = [], [], 0
-    for size, _ in PLAN:
-        starts.append(at)
-        sizes.append(size * unit)
-        at += size * unit
+    sizes = [size * unit for size, _ in PLAN]
+    starts, at = [0] * len(PLAN), 0
+    for c in sorted(range(len(PLAN)), key=lambda c: -sizes[c]):
+        starts[c] = at
+        at += sizes[c]
 
     held = []
     for (size, owner_first), begin, rows in zip(PLAN, starts, sizes):

time: 358 us -> 390 us (1.089)
  the two profiles are of different devices: /device:TPU:0 before, /device:TPU:13 now
where the time goes in v2:
time: 390 us; the launch traced here: 389 us
  waiting for transfers between devices  156 us (40%)
  Pallas kernels  112 us (29%)
  starting transfers between devices  69.4 us (18%)
  local copies, waits for them, and re-layouts  21.9 us (6%)
  matrix products  19.1 us (5%)
  other arithmetic  10.1 us (3%)
    ppermute x30, waiting for transfers between devices, spread(): moved[step] = lax.ppermute(arrays[step], axis, pairs)  118 us
    pallas_call x3, Pallas kernels, gather(): pl.pallas_call(functools.partial(gather_kernel, by_owner), grid_spec=pltp...  61.7 us
    ppermute x30, starting transfers between devices, spread(): moved[step] = lax.ppermute(arrays[step], axis, pairs)  55.1 us
    ppermute x18, waiting for transfers between devices, trade(): return lax.ppermute(value, axis, [(i, i ^ step) for i in range(size)])  37.9 us
    pallas_call x3, Pallas kernels, project(): pl.pallas_call(functools.partial(project_kernel, by_owner, min(256, rows)...  18 us
    ppermute x18, starting transfers between devices, trade(): return lax.ppermute(value, axis, [(i, i ^ step) for i in range(size)])  14.3 us
    unnamed x92, local copies, waits for them, and re-layouts  12.3 us
    pallas_call x3, Pallas kernels, arrange(): pl.pallas_call(arrange_kernel, grid=(halves, rows // tile), in_specs=[pl....  11.9 us
  transfers between devices with their start and end apart: 48, of which 18 were waited for; matrix products, arithmetic and copies ran while one was open for 8% of the time, Pallas kernels for 21%

profile of v2, /device:TPU:13, one launch (start us, length us, event | category | flops | bytes accessed | tf_op | source)
XLA Modules:
  0.0 389.1 jit_solution(10773615822985354285)
XLA Ops:
  2.0 22.1 %gather.9 = (bf16[4,192,256]{2,1,0:T(8,128)(2,1)}, bf16[4,192,256]{2,1,0:T(8,128)(2,1)}, bf16[4,192,256]{2,1,0:T(8,128)(2,1)}, bf16[4,192,256]{2,1,0:T(8,128)(2,...) custom-call(s32[1]{0:T(128)} %bitcast.place_ref, ...), custom_call_target="tpu_custom_call" | custom-call | flops 1000 | bytes 16777216 | tf_op jit(solution)/shard_map/gather/pallas_call | solution.py:115
  28.2 17.7 %gather.10 = (bf16[1024,256]{1,0:T(8,128)(2,1)}, bf16[1024,256]{1,0:T(8,128)(2,1)}, bf16[1024,256]{1,0:T(8,128)(2,1)}, bf16[1024,256]{1,0:T(8,128)(2,1)}) custom-call(s32[1]{0:T(128)} %bitcast.place_ref, s32[8,1,1024]{2,1,0:T(1,128)} %bitcast.73, bf16[8,8192,128]{2,1,0:T(8,128)(2,1)} %table_ref.5), custom_call_target="tpu_custom_call" | custom-call | flops 1000 | bytes 16777216 | tf_op jit(solution)/shard_map/gather/pallas_call | solution.py:115
  49.4 22.0 %gather.11 = (bf16[1536,256]{1,0:T(8,128)(2,1)}, bf16[1536,256]{1,0:T(8,128)(2,1)}, bf16[1536,256]{1,0:T(8,128)(2,1)}, bf16[1536,256]{1,0:T(8,128)(2,1)}) custom-call(s32[1]{0:T(128)} %bitcast.place_ref, s32[8,1,1536]{2,1,0:T(1,128)} %reshape.162.idx_ref, bf16[8,8192,128]{2,1,0:T(8,128)(2,1)} %table_ref.5), custom_call_target="tpu_custom_call" | custom-call | flops 1000 | bytes 16777216 | tf_op jit(solution)/shard_map/gather/pallas_call | solution.py:115
  91.2 19.3 %collective-permute-done.6.refs_4_ = bf16[4,192,256]{2,1,0:T(8,128)(2,1)S(1)} collective-permute-done((bf16[4,192,256]{2,1,0:T(8,128)(2,1)}, bf16[4,192,256]{2,1,0:T(8,128)(2,1)S(1)}, u32[]{:S(2)}, u32[]{:S(2)}) %collective-permute-start.6) | collective-permute-done | bytes 393248 | tf_op jit(solution)/shard_map/ppermute | solution.py:326
  110.5 12.5 %collective-permute-start.21 = (bf16[4,128,256]{2,1,0:T(8,128)(2,1)}, bf16[4,128,256]{2,1,0:T(8,128)(2,1)S(1)}, u32[]{:S(2)}, u32[]{:S(2)}) collective-permute-start(bf16[4,128,256]{2,1,0:T(8,128)(2,1)} %get-tuple-element.113), channel_id=1, source_target_pairs={{0,8},{4,12},{8,16},{12,20},{16,24},{20,28},{24,0},{28,4},{1,9},{5... | collective-permute-start | bytes 786440 | tf_op jit(solution)/shard_map/ppermute | solution.py:326
  124.2 10.7 %collective-permute-done.9.refs_7_ = bf16[4,192,256]{2,1,0:T(8,128)(2,1)} collective-permute-done((bf16[4,192,256]{2,1,0:T(8,128)(2,1)}, bf16[4,192,256]{2,1,0:T(8,128)(2,1)}, u32[]{:S(2)}, u32[]{:S(2)}) %collective-permute-start.9) | collective-permute-done | bytes 393248 | tf_op jit(solution)/shard_map/ppermute | solution.py:326
  141.7 18.0 %collective-permute-done.2.refs_3_ = bf16[8,192,256]{2,1,0:T(8,128)(2,1)S(1)} collective-permute-done((bf16[8,192,256]{2,1,0:T(8,128)(2,1)}, bf16[8,192,256]{2,1,0:T(8,128)(2,1)S(1)}, u32[]{:S(2)}, u32[]{:S(2)}) %collective-permute-start.2) | collective-permute-done | bytes 786464 | tf_op jit(solution)/shard_map/ppermute | solution.py:326
  159.7 9.0 %collective-permute-start.23 = (bf16[4,128,256]{2,1,0:T(8,128)(2,1)}, bf16[4,128,256]{2,1,0:T(8,128)(2,1)}, u32[]{:S(2)}, u32[]{:S(2)}) collective-permute-start(bf16[4,128,256]{2,1,0:T(8,128)(2,1)} %get-tuple-element.115), channel_id=1, source_target_pairs={{0,16},{4,20},{8,24},{12,28},{16,0},{20,4},{24,8},{28,12},{1,17},{... | collective-permute-start | bytes 786440 | tf_op jit(solution)/shard_map/ppermute | solution.py:326
  168.7 7.9 %collective-permute-done.28.refs_2_ = bf16[8,192,256]{2,1,0:T(8,128)(2,1)} collective-permute-done((bf16[8,192,256]{2,1,0:T(8,128)(2,1)}, bf16[8,192,256]{2,1,0:T(8,128)(2,1)}, u32[]{:S(2)}, u32[]{:S(2)}) %collective-permute-start.28) | collective-permute-done | bytes 786464 | tf_op jit(solution)/shard_map/ppermute | solution.py:326
  176.6 8.2 %collective-permute-done.29.refs_3_ = bf16[8,192,256]{2,1,0:T(8,128)(2,1)} collective-permute-done((bf16[8,192,256]{2,1,0:T(8,128)(2,1)}, bf16[8,192,256]{2,1,0:T(8,128)(2,1)}, u32[]{:S(2)}, u32[]{:S(2)}) %collective-permute-start.29) | collective-permute-done | bytes 786464 | tf_op jit(solution)/shard_map/ppermute | solution.py:326
  184.8 5.5 %collective-permute-start.26 = (bf16[4,128,256]{2,1,0:T(8,128)(2,1)}, bf16[4,128,256]{2,1,0:T(8,128)(2,1)}, u32[]{:S(2)}, u32[]{:S(2)}) collective-permute-start(bf16[4,128,256]{2,1,0:T(8,128)(2,1)} %get-tuple-element.118), channel_id=1, source_target_pairs={{0,28},{4,0},{8,4},{12,8},{16,12},{20,16},{24,20},{28,24},{1,29},{... | collective-permute-start | bytes 786440 | tf_op jit(solution)/shard_map/ppermute | solution.py:326
  193.9 6.6 %project.3 = (bf16[2,768,1024]{2,1,0:T(8,128)(2,1)}, bf16[768,512]{1,0:T(8,128)(2,1)}) custom-call(s32[1]{0:T(128)} %bitcast.place_ref, bf16[2,1024,512]{2,1,0:T(8,128)(2,1)} %convolution_convert_fusion.weight_ref, bf16[8,192,256]{2,1,0:T(8,128)(2,1)} %get-tuple-element.143.refs_0_, bf16[8,192,256]{2,1,0:T(8,128)(2,1)} %copy-done.23, ...), custom_call_target="tpu_custom_call" | custom-call | flops 1000 | bytes 6291456 | tf_op jit(solution)/shard_map/project/pallas_call | solution.py:219
  209.1 4.8 %project.4 = (bf16[2,512,1024]{2,1,0:T(8,128)(2,1)}, bf16[512,512]{1,0:T(8,128)(2,1)}) custom-call(s32[1]{0:T(128)} %bitcast.place_ref, bf16[2,1024,512]{2,1,0:T(8,128)(2,1)} %convolution_convert_fusion.weight_ref, bf16[4,128,256]{2,1,0:T(8,128)(2,1)} %get-tuple-element.148.refs_0_, bf16[4,128,256]{2,1,0:T(8,128)(2,1)} %copy-done.41, ...), custom_call_target="tpu_custom_call" | custom-call | flops 1000 | bytes 4194304 | tf_op jit(solution)/shard_map/project/pallas_call | solution.py:219
  222.0 5.3 %collective-permute-done.31 = bf16[256,512]{1,0:T(8,128)(2,1)} collective-permute-done((bf16[256,512]{1,0:T(8,128)(2,1)}, bf16[256,512]{1,0:T(8,128)(2,1)}, u32[]{:S(2)}, u32[]{:S(2)}) %collective-permute-start.31) | collective-permute-done | bytes 262176 | tf_op jit(solution)/shard_map/ppermute | solution.py:332
  231.5 5.3 %collective-permute-start.14 = (bf16[4,192,256]{2,1,0:T(8,128)(2,1)}, bf16[4,192,256]{2,1,0:T(8,128)(2,1)S(1)}, u32[]{:S(2)}, u32[]{:S(2)}) collective-permute-start(bf16[4,192,256]{2,1,0:T(8,128)(2,1)} %get-tuple-element.137), channel_id=1, source_target_pairs={{0,8},{4,12},{8,16},{12,20},{16,24},{20,28},{24,0},{28,4},{1,9},{5... | collective-permute-start | bytes 1179656 | tf_op jit(solution)/shard_map/ppermute | solution.py:326
  254.6 36.5 %collective-permute-done.15.refs_3_ = bf16[4,192,256]{2,1,0:T(8,128)(2,1)S(1)} collective-permute-done((bf16[4,192,256]{2,1,0:T(8,128)(2,1)}, bf16[4,192,256]{2,1,0:T(8,128)(2,1)S(1)}, u32[]{:S(2)}, u32[]{:S(2)}) %collective-permute-start.15) | collective-permute-done | bytes 393248 | tf_op jit(solution)/shard_map/ppermute | solution.py:326
  293.2 6.4 %collective-permute-done.16.refs_4_ = bf16[4,192,256]{2,1,0:T(8,128)(2,1)S(1)} collective-permute-done((bf16[4,192,256]{2,1,0:T(8,128)(2,1)}, bf16[4,192,256]{2,1,0:T(8,128)(2,1)S(1)}, u32[]{:S(2)}, u32[]{:S(2)}) %collective-permute-start.16) | collective-permute-done | bytes 393248 | tf_op jit(solution)/shard_map/ppermute | solution.py:326
  299.6 7.9 %collective-permute-done.18.refs_6_ = bf16[4,192,256]{2,1,0:T(8,128)(2,1)S(1)} collective-permute-done((bf16[4,192,256]{2,1,0:T(8,128)(2,1)S(1)}, bf16[4,192,256]{2,1,0:T(8,128)(2,1)S(1)}, u32[]{:S(2)}, u32[]{:S(2)}) %collective-permute-start.18) | collective-permute-done | bytes 393248 | tf_op jit(solution)/shard_map/ppermute | solution.py:326
  309.0 6.5 %project.5 = (bf16[2,768,1024]{2,1,0:T(8,128)(2,1)}, bf16[768,512]{1,0:T(8,128)(2,1)}) custom-call(s32[1]{0:T(128)} %bitcast.place_ref, bf16[2,1024,512]{2,1,0:T(8,128)(2,1)} %convolution_convert_fusion.weight_ref, bf16[4,192,256]{2,1,0:T(8,128)(2,1)} %get-tuple-element.158.refs_0_, bf16[4,192,256]{2,1,0:T(8,128)(2,1)} %copy-done.34, ...), custom_call_target="tpu_custom_call" | custom-call | flops 1000 | bytes 6291456 | tf_op jit(solution)/shard_map/project/pallas_call | solution.py:219
  327.6 5.1 %collective-permute-done.34 = bf16[256,512]{1,0:T(8,128)(2,1)S(1)} collective-permute-done((bf16[256,512]{1,0:T(8,128)(2,1)S(1)}, bf16[256,512]{1,0:T(8,128)(2,1)S(1)}, u32[]{:S(2)}, u32[]{:S(2)}) %collective-permute-start.34) | collective-permute-done | bytes 262176 | tf_op jit(solution)/shard_map/ppermute | solution.py:332
  333.8 7.3 %collective-permute-done.43 = bf16[384,512]{1,0:T(8,128)(2,1)S(1)} collective-permute-done((bf16[384,512]{1,0:T(8,128)(2,1)S(1)}, bf16[384,512]{1,0:T(8,128)(2,1)S(1)}, u32[]{:S(2)}, u32[]{:S(2)}) %collective-permute-start.43) | collective-permute-done | bytes 393248 | tf_op jit(solution)/shard_map/ppermute | solution.py:332
  342.3 7.2 %collective-permute-done.40 = bf16[384,512]{1,0:T(8,128)(2,1)S(1)} collective-permute-done((bf16[384,512]{1,0:T(8,128)(2,1)S(1)}, bf16[384,512]{1,0:T(8,128)(2,1)S(1)}, u32[]{:S(2)}, u32[]{:S(2)}) %collective-permute-start.40) | collective-permute-done | bytes 393248 | tf_op jit(solution)/shard_map/ppermute | solution.py:332
  359.8 4.5 %arrange.5 = bf16[768,2048]{1,0:T(8,128)(2,1)S(1)} custom-call(bf16[2,768,1024]{2,1,0:T(8,128)(2,1)S(1)} %copy-done.8, bf16[2,1024,1024]{2,1,0:T(8,128)(2,1)S(1)} %copy-done.5), custom_call_target="tpu_custom_call" | custom-call | flops 1000 | bytes 6291456 | tf_op jit(solution)/shard_map/arrange/pallas_call | solution.py:252
  373.0 9.2 %collective-permute-done.46 = bf16[384,512]{1,0:T(8,128)(2,1)S(1)} collective-permute-done((bf16[384,512]{1,0:T(8,128)(2,1)S(1)}, bf16[384,512]{1,0:T(8,128)(2,1)S(1)}, u32[]{:S(2)}, u32[]{:S(2)}) %collective-permute-start.46) | collective-permute-done | bytes 393248 | tf_op jit(solution)/shard_map/ppermute | solution.py:332
  (233 shorter events, 123.0 us)
Async XLA Ops:
  24.1 49.5 %collective-permute-start.3 = (bf16[4,192,256]{2,1,0:T(8,128)(2,1)}, bf16[4,192,256]{2,1,0:T(8,128)(2,1)S(1)}, u32[]{:S(2)}, u32[]{:S(2)}) collective-permute-start(bf16[4,192,256]{2,1,0:T(8,128)(2,1)} %get-tuple-element.89), channel_id=1, source_target_pairs={{0,4},{4,8},{8,12},{12,16},{16,20},{20,24},{24,28},{28,0},{1,5},{5... | collective-permute-start | bytes 1179656 | tf_op jit(solution)/shard_map/ppermute | solution.py:326
  25.3 49.4 %collective-permute-start.4 = (bf16[4,192,256]{2,1,0:T(8,128)(2,1)}, bf16[4,192,256]{2,1,0:T(8,128)(2,1)S(1)}, u32[]{:S(2)}, u32[]{:S(2)}) collective-permute-start(bf16[4,192,256]{2,1,0:T(8,128)(2,1)} %get-tuple-element.90), channel_id=1, source_target_pairs={{0,8},{4,12},{8,16},{12,20},{16,24},{20,28},{24,0},{28,4},{1,9},{5... | collective-permute-start | bytes 1179656 | tf_op jit(solution)/shard_map/ppermute | solution.py:326
  26.6 49.6 %collective-permute-start.5 = (bf16[4,192,256]{2,1,0:T(8,128)(2,1)}, bf16[4,192,256]{2,1,0:T(8,128)(2,1)S(1)}, u32[]{:S(2)}, u32[]{:S(2)}) collective-permute-start(bf16[4,192,256]{2,1,0:T(8,128)(2,1)} %get-tuple-element.91), channel_id=1, source_target_pairs={{0,12},{4,16},{8,20},{12,24},{16,28},{20,0},{24,4},{28,8},{1,13},{... | collective-permute-start | bytes 1179656 | tf_op jit(solution)/shard_map/ppermute | solution.py:326
  45.9 31.3 %collective-permute-start.10 = (bf16[8,128,256]{2,1,0:T(8,128)(2,1)}, bf16[8,128,256]{2,1,0:T(8,128)(2,1)S(1)}, u32[]{:S(2)}, u32[]{:S(2)}) collective-permute-start(bf16[8,128,256]{2,1,0:T(8,128)(2,1)} %bitcast.81), channel_id=1, source_target_pairs={{0,1},{1,2},{2,3},{3,0},{4,5},{5,6},{6,7},{7,4},{8,9},{9,10},{10,1... | collective-permute-start | bytes 1572872 | tf_op jit(solution)/shard_map/ppermute | solution.py:326
  48.4 29.9 %collective-permute-start.11 = (bf16[8,128,256]{2,1,0:T(8,128)(2,1)}, bf16[8,128,256]{2,1,0:T(8,128)(2,1)S(1)}, u32[]{:S(2)}, u32[]{:S(2)}) collective-permute-start(bf16[8,128,256]{2,1,0:T(8,128)(2,1)} %bitcast.80), channel_id=1, source_target_pairs={{0,2},{1,3},{2,0},{3,1},{4,6},{5,7},{6,4},{7,5},{8,10},{9,11},{10,... | collective-permute-start | bytes 1572872 | tf_op jit(solution)/shard_map/ppermute | solution.py:326
  74.7 35.8 %collective-permute-start.6 = (bf16[4,192,256]{2,1,0:T(8,128)(2,1)}, bf16[4,192,256]{2,1,0:T(8,128)(2,1)S(1)}, u32[]{:S(2)}, u32[]{:S(2)}) collective-permute-start(bf16[4,192,256]{2,1,0:T(8,128)(2,1)} %get-tuple-element.92), channel_id=1, source_target_pairs={{0,16},{4,20},{8,24},{12,28},{16,0},{20,4},{24,8},{28,12},{1,17},{... | collective-permute-start | bytes 1179656 | tf_op jit(solution)/shard_map/ppermute | solution.py:326
  76.2 34.3 %collective-permute-start.7 = (bf16[4,192,256]{2,1,0:T(8,128)(2,1)}, bf16[4,192,256]{2,1,0:T(8,128)(2,1)S(1)}, u32[]{:S(2)}, u32[]{:S(2)}) collective-permute-start(bf16[4,192,256]{2,1,0:T(8,128)(2,1)} %get-tuple-element.93), channel_id=1, source_target_pairs={{0,20},{4,24},{8,28},{12,0},{16,4},{20,8},{24,12},{28,16},{1,21},{... | collective-permute-start | bytes 1179656 | tf_op jit(solution)/shard_map/ppermute | solution.py:326
  77.2 45.9 %collective-permute-start.8 = (bf16[4,192,256]{2,1,0:T(8,128)(2,1)}, bf16[4,192,256]{2,1,0:T(8,128)(2,1)}, u32[]{:S(2)}, u32[]{:S(2)}) collective-permute-start(bf16[4,192,256]{2,1,0:T(8,128)(2,1)} %get-tuple-element.94), channel_id=1, source_target_pairs={{0,24},{4,28},{8,0},{12,4},{16,8},{20,12},{24,16},{28,20},{1,25},{... | collective-permute-start | bytes 1179656 | tf_op jit(solution)/shard_map/ppermute | solution.py:326
  78.3 56.5 %collective-permute-start.9 = (bf16[4,192,256]{2,1,0:T(8,128)(2,1)}, bf16[4,192,256]{2,1,0:T(8,128)(2,1)}, u32[]{:S(2)}, u32[]{:S(2)}) collective-permute-start(bf16[4,192,256]{2,1,0:T(8,128)(2,1)} %get-tuple-element.95), channel_id=1, source_target_pairs={{0,28},{4,0},{8,4},{12,8},{16,12},{20,16},{24,20},{28,24},{1,29},{... | collective-permute-start | bytes 1179656 | tf_op jit(solution)/shard_map/ppermute | solution.py:326
  82.6 58.8 %collective-permute-start = (bf16[8,192,256]{2,1,0:T(8,128)(2,1)}, bf16[8,192,256]{2,1,0:T(8,128)(2,1)S(1)}, u32[]{:S(2)}, u32[]{:S(2)}) collective-permute-start(bf16[8,192,256]{2,1,0:T(8,128)(2,1)} %bitcast.9), channel_id=1, source_target_pairs={{0,1},{1,2},{2,3},{3,0},{4,5},{5,6},{6,7},{7,4},{8,9},{9,10},{10,1... | collective-permute-start | bytes 2359304 | tf_op jit(solution)/shard_map/ppermute | solution.py:326
  110.5 28.4 %collective-permute-start.20 = (bf16[4,128,256]{2,1,0:T(8,128)(2,1)}, bf16[4,128,256]{2,1,0:T(8,128)(2,1)S(1)}, u32[]{:S(2)}, u32[]{:S(2)}) collective-permute-start(bf16[4,128,256]{2,1,0:T(8,128)(2,1)} %get-tuple-element.112), channel_id=1, source_target_pairs={{0,4},{4,8},{8,12},{12,16},{16,20},{20,24},{24,28},{28,0},{1,5},{5... | collective-permute-start | bytes 786440 | tf_op jit(solution)/shard_map/ppermute | solution.py:326
  110.5 29.7 %collective-permute-start.21 = (bf16[4,128,256]{2,1,0:T(8,128)(2,1)}, bf16[4,128,256]{2,1,0:T(8,128)(2,1)S(1)}, u32[]{:S(2)}, u32[]{:S(2)}) collective-permute-start(bf16[4,128,256]{2,1,0:T(8,128)(2,1)} %get-tuple-element.113), channel_id=1, source_target_pairs={{0,8},{4,12},{8,16},{12,20},{16,24},{20,28},{24,0},{28,4},{1,9},{5... | collective-permute-start | bytes 786440 | tf_op jit(solution)/shard_map/ppermute | solution.py:326
  139.0 29.7 %collective-permute-start.27 = (bf16[8,192,256]{2,1,0:T(8,128)(2,1)}, bf16[8,192,256]{2,1,0:T(8,128)(2,1)S(1)}, u32[]{:S(2)}, u32[]{:S(2)}) collective-permute-start(bf16[8,192,256]{2,1,0:T(8,128)(2,1)} %get-tuple-element.128), channel_id=1, source_target_pairs={{0,1},{1,2},{2,3},{3,0},{4,5},{5,6},{6,7},{7,4},{8,9},{9,10},{10,1... | collective-permute-start | bytes 2359304 | tf_op jit(solution)/shard_map/ppermute | solution.py:326
  140.3 36.4 %collective-permute-start.28 = (bf16[8,192,256]{2,1,0:T(8,128)(2,1)}, bf16[8,192,256]{2,1,0:T(8,128)(2,1)}, u32[]{:S(2)}, u32[]{:S(2)}) collective-permute-start(bf16[8,192,256]{2,1,0:T(8,128)(2,1)} %get-tuple-element.129), channel_id=1, source_target_pairs={{0,2},{1,3},{2,0},{3,1},{4,6},{5,7},{6,4},{7,5},{8,10},{9,11},{10,... | collective-permute-start | bytes 2359304 | tf_op jit(solution)/shard_map/ppermute | solution.py:326
  141.4 43.4 %collective-permute-start.29 = (bf16[8,192,256]{2,1,0:T(8,128)(2,1)}, bf16[8,192,256]{2,1,0:T(8,128)(2,1)}, u32[]{:S(2)}, u32[]{:S(2)}) collective-permute-start(bf16[8,192,256]{2,1,0:T(8,128)(2,1)} %get-tuple-element.130), channel_id=1, source_target_pairs={{0,3},{1,0},{2,1},{3,2},{4,7},{5,4},{6,5},{7,6},{8,11},{9,8},{10,9... | collective-permute-start | bytes 2359304 | tf_op jit(solution)/shard_map/ppermute | solution.py:326
  141.4 67.6 %collective-permute-start.22 = (bf16[4,128,256]{2,1,0:T(8,128)(2,1)}, bf16[4,128,256]{2,1,0:T(8,128)(2,1)}, u32[]{:S(2)}, u32[]{:S(2)}) collective-permute-start(bf16[4,128,256]{2,1,0:T(8,128)(2,1)} %get-tuple-element.114), channel_id=1, source_target_pairs={{0,12},{4,16},{8,20},{12,24},{16,28},{20,0},{24,4},{28,8},{1,13},{... | collective-permute-start | bytes 786440 | tf_op jit(solution)/shard_map/ppermute | solution.py:326
  159.7 49.4 %collective-permute-start.23 = (bf16[4,128,256]{2,1,0:T(8,128)(2,1)}, bf16[4,128,256]{2,1,0:T(8,128)(2,1)}, u32[]{:S(2)}, u32[]{:S(2)}) collective-permute-start(bf16[4,128,256]{2,1,0:T(8,128)(2,1)} %get-tuple-element.115), channel_id=1, source_target_pairs={{0,16},{4,20},{8,24},{12,28},{16,0},{20,4},{24,8},{28,12},{1,17},{... | collective-permute-start | bytes 786440 | tf_op jit(solution)/shard_map/ppermute | solution.py:326
  168.7 40.4 %collective-permute-start.24 = (bf16[4,128,256]{2,1,0:T(8,128)(2,1)}, bf16[4,128,256]{2,1,0:T(8,128)(2,1)}, u32[]{:S(2)}, u32[]{:S(2)}) collective-permute-start(bf16[4,128,256]{2,1,0:T(8,128)(2,1)} %get-tuple-element.116), channel_id=1, source_target_pairs={{0,20},{4,24},{8,28},{12,0},{16,4},{20,8},{24,12},{28,16},{1,21},{... | collective-permute-start | bytes 786440 | tf_op jit(solution)/shard_map/ppermute | solution.py:326
  176.6 32.4 %collective-permute-start.25 = (bf16[4,128,256]{2,1,0:T(8,128)(2,1)}, bf16[4,128,256]{2,1,0:T(8,128)(2,1)}, u32[]{:S(2)}, u32[]{:S(2)}) collective-permute-start(bf16[4,128,256]{2,1,0:T(8,128)(2,1)} %get-tuple-element.117), channel_id=1, source_target_pairs={{0,24},{4,28},{8,0},{12,4},{16,8},{20,12},{24,16},{28,20},{1,25},{... | collective-permute-start | bytes 786440 | tf_op jit(solution)/shard_map/ppermute | solution.py:326
  236.8 54.3 %collective-permute-start.15 = (bf16[4,192,256]{2,1,0:T(8,128)(2,1)}, bf16[4,192,256]{2,1,0:T(8,128)(2,1)S(1)}, u32[]{:S(2)}, u32[]{:S(2)}) collective-permute-start(bf16[4,192,256]{2,1,0:T(8,128)(2,1)} %get-tuple-element.138), channel_id=1, source_target_pairs={{0,12},{4,16},{8,20},{12,24},{16,28},{20,0},{24,4},{28,8},{1,13},{... | collective-permute-start | bytes 1179656 | tf_op jit(solution)/shard_map/ppermute | solution.py:326
  245.5 54.0 %collective-permute-start.16 = (bf16[4,192,256]{2,1,0:T(8,128)(2,1)}, bf16[4,192,256]{2,1,0:T(8,128)(2,1)S(1)}, u32[]{:S(2)}, u32[]{:S(2)}) collective-permute-start(bf16[4,192,256]{2,1,0:T(8,128)(2,1)} %get-tuple-element.139), channel_id=1, source_target_pairs={{0,16},{4,20},{8,24},{12,28},{16,0},{20,4},{24,8},{28,12},{1,17},{... | collective-permute-start | bytes 1179656 | tf_op jit(solution)/shard_map/ppermute | solution.py:326
  247.0 52.6 %collective-permute-start.17 = (bf16[4,192,256]{2,1,0:T(8,128)(2,1)}, bf16[4,192,256]{2,1,0:T(8,128)(2,1)S(1)}, u32[]{:S(2)}, u32[]{:S(2)}) collective-permute-start(bf16[4,192,256]{2,1,0:T(8,128)(2,1)} %get-tuple-element.140), channel_id=1, source_target_pairs={{0,20},{4,24},{8,28},{12,0},{16,4},{20,8},{24,12},{28,16},{1,21},{... | collective-permute-start | bytes 1179656 | tf_op jit(solution)/shard_map/ppermute | solution.py:326
  252.1 55.4 %collective-permute-start.18 = (bf16[4,192,256]{2,1,0:T(8,128)(2,1)S(1)}, bf16[4,192,256]{2,1,0:T(8,128)(2,1)S(1)}, u32[]{:S(2)}, u32[]{:S(2)}) collective-permute-start(bf16[4,192,256]{2,1,0:T(8,128)(2,1)S(1)} %copy-done.45), channel_id=1, source_target_pairs={{0,24},{4,28},{8,0},{12,4},{16,8},{20,12},{24,16},{28,20},{1,25},{... | collective-permute-start | bytes 1179656 | tf_op jit(solution)/shard_map/ppermute | solution.py:326
  254.5 53.0 %collective-permute-start.19 = (bf16[4,192,256]{2,1,0:T(8,128)(2,1)S(1)}, bf16[4,192,256]{2,1,0:T(8,128)(2,1)S(1)}, u32[]{:S(2)}, u32[]{:S(2)}) collective-permute-start(bf16[4,192,256]{2,1,0:T(8,128)(2,1)S(1)} %copy-done.44), channel_id=1, source_target_pairs={{0,28},{4,0},{8,4},{12,8},{16,12},{20,16},{24,20},{28,24},{1,29},{... | collective-permute-start | bytes 1179656 | tf_op jit(solution)/shard_map/ppermute | solution.py:326
  (71 other events, 972.7 us)
